TPU v7x, 256 devices: a whole 4x4x8 slice. The times are simulated.
256 devices in a mesh: blk: 32 (over x, z), sub: 8 (over y, core).
Axes of the slice: x: 4, y: 4, z: 8, core: 2. Of those that a mesh axis runs over, the one named last changes fastest.
Arguments:
- features: float32 [131072, 128], P(('blk', 'sub')), may hold values from -6 to 6
- weight: float32 [128, 128], replicated, may hold values from -0.5 to 0.5
- bias: float32 [128], replicated, may hold values from -3 to 3
- adj_tiles: float32 [16384, 128, 128], P(('blk', 'sub')), may hold values from 0 to 0.046875
- tile_rows: int32 [16384], P(('blk', 'sub')), may hold values from 0 to 1023, as said below
- tile_cols: int32 [16384], P(('blk', 'sub')), may hold values from 0 to 1023, as said below
- tile_counts: int32 [8192], P(('blk', 'sub')), may hold values from 0 to 2, as said below
- cotangent: float32 [131072, 128], P(('blk', 'sub')), may hold values from -6 to 6
Outputs:
- activation: float32 [131072, 128], P(('blk', 'sub'))
- grad_features: float32 [131072, 128], P(('blk', 'sub'))
- grad_weight: float32 [128, 128], replicated
- grad_bias: float32 [128], replicated
Inputs may be any that keep to these rules, and one draw needn't show every extreme that they name: `tile_rows`: a slot's row block is one of the 32 blocks of the 8 devices that share the holding device's blk index. `tile_cols`: slot k of a device has its column block in group k // 2, the 32 blocks of the devices with blk index k // 2. `tile_counts`: the live slots of a group are its first ones; some device has all slots live in every draw.
All inputs are finite; a program needn't handle non-finite values.
Results may differ from a plain program's by a relative error of at most 0.00023.
Values sent between devices are 32-bit elements; how exact they have to be, the bound alone decides.
A program may use at most 128 MiB of HBM per device.

v0:
```python
import math

import jax
import jax.numpy as jnp
from jax import lax
from jax.sharding import Mesh
from jax.sharding import PartitionSpec as P

BS = 128
CAP = 2
BLK_SUB = ("blk_0", "blk_1", "sub_0", "sub_1")
BLK = ("blk_0", "blk_1")
SUB = ("sub_0", "sub_1")


def filled_up(lines, peers):
    spare = -lines.shape[0] % peers
    if not spare:
        return lines
    return jnp.concatenate([lines, jnp.zeros((spare, *lines.shape[1:]), lines.dtype)])


def copy_for_each(value, axis):
    peers = lax.axis_size(axis)
    return lax.all_to_all(
        jnp.broadcast_to(value[None], (peers, *value.shape)), axis, 0, 0, tiled=True
    )


def in_order(pieces, dim):
    pieces = jnp.moveaxis(pieces, 0, dim)
    lengths = pieces.shape
    return pieces.reshape(*lengths[:dim], lengths[dim] * lengths[dim + 1], *lengths[dim + 2 :])


def whole_of(value, axes, dim):
    far, near = axes
    pieces = copy_for_each(copy_for_each(value, far), near)
    return in_order(pieces.swapaxes(0, 1).reshape(-1, *value.shape), dim)


def cut_along(value, dim, peers):
    lengths = value.shape
    pieces = value.reshape(*lengths[:dim], peers, lengths[dim] // peers, *lengths[dim + 1 :])
    return jnp.moveaxis(pieces, dim, 0)


def summed_on_arrival(value, axis, dim):
    peers = lax.axis_size(axis)
    pieces = lax.all_to_all(cut_along(value, dim, peers), axis, 0, 0, tiled=True)
    return jnp.sum(pieces, axis=0)


def summed_rows(value, axes, dim):
    far, near = axes
    pieces = cut_along(value, dim, lax.axis_size(far))
    nearer = summed_on_arrival(pieces, near, dim + 1)
    arrived = lax.all_to_all(nearer, far, split_axis=0, concat_axis=0, tiled=True)
    return arrived.sum(axis=0)


def nested_sum(value, axes):
    padded = filled_up(value, lax.axis_size(axes[0]) * lax.axis_size(axes[1]))
    whole = whole_of(summed_rows(padded, axes, 0), axes, 0)
    return lax.slice_in_dim(whole, 0, len(value)).reshape(value.shape)


def together(arrays, axis):
    vector, at, finished = (jnp.concatenate([a.reshape(-1) for a in arrays]), 0, [])
    so_far = nested_sum(vector, axis)
    for a in arrays:
        finished.append(so_far[at : at + a.size].reshape(a.shape))
        at += a.size
    return tuple(finished)


def sum_params(part_weight, part_bias):
    return together((part_weight, part_bias), (("blk_0", "blk_1"), ("sub_0", "sub_1")))


def body(features, weight, bias, adj_tiles, tile_rows, tile_cols, tile_counts, cotangent):
    block_count = lax.axis_size(BLK)
    sub_count = lax.axis_size(SUB)
    group_index = lax.axis_index(BLK)
    width = features.shape[1]
    own_blocks = features.shape[0] // BS
    group_size = own_blocks * sub_count
    slot_count = adj_tiles.shape[0]
    scale = 1.0 / math.sqrt(features.shape[0] * block_count * sub_count)
    slot_ids = jnp.arange(slot_count, dtype=jnp.int32)
    target_group = slot_ids // CAP
    alive_mask = (slot_ids % CAP < tile_counts[target_group]).astype(jnp.float32)
    masked_tiles = adj_tiles * alive_mask[:, None, None]
    row_local = tile_rows - group_index * group_size
    col_local = tile_cols - target_group * group_size
    block_ids = jnp.arange(group_size, dtype=jnp.int32)
    row_onehot = (block_ids[:, None] == row_local[None, :]).astype(jnp.float32)
    known_ids = lax.all_to_all(
        col_local.reshape(block_count, CAP), BLK, split_axis=0, concat_axis=0, tiled=True
    ).reshape(-1)

    def aggregate(values):
        gathered = whole_of(values, ("sub_0", "sub_1"), 0).reshape(group_size, BS, width)
        pushed = jnp.einsum(
            "kji,kjf->kif", masked_tiles, gathered[row_local], precision=lax.Precision.HIGHEST
        )
        answer = gathered[known_ids].reshape(block_count, CAP, BS, width)
        arrived, fetched = (
            lax.all_to_all(
                pushed.reshape(block_count, CAP, BS, width),
                BLK,
                split_axis=0,
                concat_axis=0,
                tiled=True,
            ),
            lax.all_to_all(answer, BLK, split_axis=0, concat_axis=0, tiled=True),
        )
        fetched = fetched.reshape(slot_count, BS, width)
        pulled = jnp.einsum("kij,kjf->kif", masked_tiles, fetched, precision=lax.Precision.HIGHEST)
        in_onehot = (block_ids[:, None] == known_ids[None, :]).astype(jnp.float32)
        summed = jnp.dot(
            in_onehot, arrived.reshape(slot_count, BS * width), precision=lax.Precision.HIGHEST
        )
        summed = summed + jnp.dot(
            row_onehot, pulled.reshape(slot_count, BS * width), precision=lax.Precision.HIGHEST
        )
        return summed_on_arrival(summed.reshape(group_size * BS, width), SUB, 0)

    mixed = jnp.dot(features, weight, precision=lax.Precision.HIGHEST)
    pre = aggregate(mixed) + bias
    sigma = jax.nn.sigmoid(pre)
    activation = pre * sigma
    grad_pre = cotangent * sigma * (1.0 + pre * (1.0 - sigma))
    grad_mixed = aggregate(grad_pre)
    grad_features = jnp.dot(grad_mixed, weight.T, precision=lax.Precision.HIGHEST)
    grad_weight, grad_bias = sum_params(
        jnp.dot(features.T, grad_mixed, precision=lax.Precision.HIGHEST) * scale,
        jnp.sum(grad_pre, axis=0) * scale,
    )
    return (activation, grad_features, grad_weight, grad_bias)


def solution(mesh):
    finer = Mesh(mesh.devices.reshape(4, 8, 4, 2), ("blk_0", "blk_1", "sub_0", "sub_1"))
    return jax.shard_map(
        body,
        mesh=finer,
        in_specs=(
            P(BLK_SUB, None),
            P(),
            P(),
            P(BLK_SUB, None, None),
            P(BLK_SUB),
            P(BLK_SUB),
            P(BLK_SUB),
            P(BLK_SUB, None),
        ),
        out_specs=(P(BLK_SUB, None), P(BLK_SUB, None), P(), P()),
        check_vma=False,
    )
```

profile of v0, /device:TPU:1, one launch (start us, length us, event | category | flops | bytes accessed | tf_op | source)
XLA Modules:
  0.0 637.8 jit_solution(9191543659964028968)
XLA Ops:
  0.6 0.7 fusion.29
  1.3 0.7 all_to_all.52
  2.1 11.9 %all-to-all-start = ((s32[32,1,2]{2,1,0:T(1,128)}), s32[32,1,2]{2,1,0:T(1,128)S(1)}, u32[]{:S(2)}, u32[]{:S(2)}) async-start(s32[32,1,2]{2,1,0:T(1,128)} %bitcast), calls=%async_computation | async-start | bytes 32768 | tf_op jit(solution)/shard_map/all_to_all | solution.py:98
  13.9 1.2 fusion.33
  15.1 7.4 %all-to-all-done = s32[32,1,2]{2,1,0:T(1,128)S(1)} async-done(((s32[32,1,2]{2,1,0:T(1,128)}), s32[32,1,2]{2,1,0:T(1,128)S(1)}, u32[]{:S(2)}, u32[]{:S(2)}) %all-to-all-start) | async-done | bytes 288 | tf_op jit(solution)/shard_map/all_to_all | solution.py:98
  22.5 1.0 broadcast_in_dim.18
  23.5 4.2 all-to-all-start.1
  27.7 0.1 reshape.156
  27.9 12.4 %all-to-all-done.1 = f32[4,512,128]{2,1,0:T(8,128)S(1)} async-done(((f32[4,512,128]{2,1,0:T(8,128)}), f32[4,512,128]{2,1,0:T(8,128)S(1)}, u32[]{:S(2)}, u32[]{:S(2)}) %all-to-all-start.1) | async-done | bytes 1048608 | tf_op jit(solution)/shard_map/all_to_all | solution.py:25
  40.2 0.1 broadcast_in_dim.19
  40.4 8.6 %all_to_all.84 = f32[2,4,512,128]{3,2,1,0:T(8,128)S(1)} all-to-all(f32[2,4,512,128]{3,2,1,0:T(8,128)S(1)} %broadcast_in_dim.19), channel_id=1, replica_groups=mesh['blk_0'=4,'blk_1'=8,'sub_0'=4,'sub_1'=2] {'sub_1'}, dimensions={0} | all-to-all | bytes 4194304 | tf_op jit(solution)/shard_map/all_to_all | solution.py:25
  49.0 0.1 copy.24
  49.1 2.8 gather_fusion.2
  51.9 5.0 all-to-all-start.4
  56.9 0.8 gather_fusion
  57.8 2.8 gather_fusion.1
  60.5 12.3 %fusion.16 = f32[64,128,128]{2,1,0:T(8,128)} fusion(f32[64,128,128]{2,1,0:T(8,128)} %gather_fusion.1, f32[64,128,128]{2,1,0:T(8,128)} %param.11, f32[64]{0:T(128)S(1)} %compare_convert_fusion), kind=kOutput, calls=%fused_computation.23 | convolution fusion | flops 1611661312 | bytes 12583168 | tf_op jit(solution)/shard_map/kji,kjf->kif/dot_general | solution.py:104
  72.8 76.6 %all-to-all-done.4 = f32[32,2,128,128]{3,2,1,0:T(8,128)} async-done(((f32[32,2,128,128]{3,2,1,0:T(8,128)}), f32[32,2,128,128]{3,2,1,0:T(8,128)}, u32[]{:S(2)}, u32[]{:S(2)}) %all-to-all-start.4) | async-done | bytes 4194336 | tf_op jit(solution)/shard_map/all_to_all | solution.py:116
  149.4 9.8 %all-to-all-start.3 = ((f32[32,2,128,128]{3,2,1,0:T(8,128)}), f32[32,2,128,128]{3,2,1,0:T(8,128)}, u32[]{:S(2)}, u32[]{:S(2)}) async-start(f32[32,2,128,128]{3,2,1,0:T(8,128)} %bitcast.58), calls=%async_computation.3 | async-start | bytes 8388608 | tf_op jit(solution)/shard_map/all_to_all | solution.py:109
  159.2 0.5 broadcast.145
  159.8 0.7 reduce.6
  160.5 0.1 eq.17
  160.6 9.9 %fusion.14 = f32[64,128,128]{2,1,0:T(8,128)} fusion(f32[64,128,128]{2,1,0:T(8,128)} %bitcast.8, f32[64,128,128]{2,1,0:T(8,128)} %param.11, f32[64]{0:T(128)S(1)} %compare_convert_fusion), kind=kOutput, calls=%fused_computation.21 | convolution fusion | flops 1611661312 | bytes 12583168 | tf_op jit(solution)/shard_map/kij,kjf->kif/dot_general | solution.py:119
  170.4 82.8 %all-to-all-done.3 = f32[32,2,128,128]{3,2,1,0:T(8,128)} async-done(((f32[32,2,128,128]{3,2,1,0:T(8,128)}), f32[32,2,128,128]{3,2,1,0:T(8,128)}, u32[]{:S(2)}, u32[]{:S(2)}) %all-to-all-start.3) | async-done | bytes 4194336 | tf_op jit(solution)/shard_map/all_to_all | solution.py:109
  253.3 6.2 fusion.7
  259.5 4.6 convolution_add_fusion.1
  264.1 1.5 reshape_reshape.12
  265.6 33.4 %all_to_all.85 = f32[8,512,128]{2,1,0:T(8,128)S(1)} all-to-all(f32[8,512,128]{2,1,0:T(8,128)} %reshape_reshape.12), channel_id=1, replica_groups=mesh['blk_0'=4,'blk_1'=8,'sub_0'=4,'sub_1'=2] {'sub_0','sub_1'}, dimensions={0} | all-to-all | bytes 4194304 | tf_op jit(solution)/shard_map/all_to_all | solution.py:50
  299.0 0.1 reduce_sum.45
  299.1 0.8 fusion.32
  299.9 0.1 broadcast_in_dim.21
  300.0 16.6 %all_to_all.86 = f32[4,512,128]{2,1,0:T(8,128)S(1)} all-to-all(f32[4,512,128]{2,1,0:T(8,128)S(1)} %broadcast_in_dim.21), channel_id=1, replica_groups=mesh['blk_0'=4,'blk_1'=8,'sub_0'=4,'sub_1'=2] {'sub_0'}, dimensions={0} | all-to-all | bytes 2097152 | tf_op jit(solution)/shard_map/all_to_all | solution.py:25
  316.6 0.1 broadcast_in_dim.22
  316.7 6.9 %all_to_all.87 = f32[2,4,512,128]{3,2,1,0:T(8,128)S(1)} all-to-all(f32[2,4,512,128]{3,2,1,0:T(8,128)S(1)} %broadcast_in_dim.22), channel_id=1, replica_groups=mesh['blk_0'=4,'blk_1'=8,'sub_0'=4,'sub_1'=2] {'sub_1'}, dimensions={0} | all-to-all | bytes 4194304 | tf_op jit(solution)/shard_map/all_to_all | solution.py:25
  323.7 0.1 copy.26
  323.8 2.8 gather_fusion.3
  326.6 12.3 %fusion.12 = f32[64,128,128]{2,1,0:T(8,128)} fusion(f32[64,128,128]{2,1,0:T(8,128)} %gather_fusion.3, f32[64,128,128]{2,1,0:T(8,128)} %param.11, f32[64]{0:T(128)S(1)} %compare_convert_fusion), kind=kOutput, calls=%fused_computation.19 | convolution fusion | flops 1611661312 | bytes 12583168 | tf_op jit(solution)/shard_map/kji,kjf->kif/dot_general | solution.py:104
  338.9 4.9 all-to-all-start.8
  343.8 2.8 gather_fusion.4
  346.5 91.1 %all-to-all-done.8 = f32[32,2,128,128]{3,2,1,0:T(8,128)} async-done(((f32[32,2,128,128]{3,2,1,0:T(8,128)}), f32[32,2,128,128]{3,2,1,0:T(8,128)}, u32[]{:S(2)}, u32[]{:S(2)}) %all-to-all-start.8) | async-done | bytes 4194336 | tf_op jit(solution)/shard_map/all_to_all | solution.py:109
  437.6 8.3 %all-to-all-start.9 = ((f32[32,2,128,128]{3,2,1,0:T(8,128)}), f32[32,2,128,128]{3,2,1,0:T(8,128)}, u32[]{:S(2)}, u32[]{:S(2)}) async-start(f32[32,2,128,128]{3,2,1,0:T(8,128)} %bitcast.59), calls=%async_computation.9 | async-start | bytes 8388608 | tf_op jit(solution)/shard_map/all_to_all | solution.py:116
  445.9 6.0 fusion.2
  452.0 86.4 %all-to-all-done.9 = f32[32,2,128,128]{3,2,1,0:T(8,128)} async-done(((f32[32,2,128,128]{3,2,1,0:T(8,128)}), f32[32,2,128,128]{3,2,1,0:T(8,128)}, u32[]{:S(2)}, u32[]{:S(2)}) %all-to-all-start.9) | async-done | bytes 4194336 | tf_op jit(solution)/shard_map/all_to_all | solution.py:116
  538.4 6.8 %fusion.10 = f32[64,128,128]{2,1,0:T(8,128)S(1)} fusion(f32[64,128,128]{2,1,0:T(8,128)} %bitcast.14, f32[64,128,128]{2,1,0:T(8,128)} %param.11, f32[64]{0:T(128)S(1)} %compare_convert_fusion), kind=kOutput, calls=%fused_computation.17 | convolution fusion | flops 1611661312 | bytes 12583168 | tf_op jit(solution)/shard_map/kij,kjf->kif/dot_general | solution.py:119
  545.3 5.4 convolution_add_fusion
  550.7 2.7 reshape_reshape.13
  553.4 9.1 %all-to-all-start.10 = ((f32[8,512,128]{2,1,0:T(8,128)}), f32[8,512,128]{2,1,0:T(8,128)S(1)}, u32[]{:S(2)}, u32[]{:S(2)}) async-start(f32[8,512,128]{2,1,0:T(8,128)} %reshape_reshape.13), calls=%async_computation.10 | async-start | bytes 4194304 | tf_op jit(solution)/shard_map/all_to_all | solution.py:50
  562.5 26.2 %all-to-all-done.10 = f32[8,512,128]{2,1,0:T(8,128)S(1)} async-done(((f32[8,512,128]{2,1,0:T(8,128)}), f32[8,512,128]{2,1,0:T(8,128)S(1)}, u32[]{:S(2)}, u32[]{:S(2)}) %all-to-all-start.10) | async-done | bytes 2097184 | tf_op jit(solution)/shard_map/all_to_all | solution.py:50
  588.7 0.1 reduce_sum.46
  588.8 0.6 fusion.22
  589.4 0.1 copy.28
  589.5 0.2 reshape_reshape.14
  589.8 8.6 %all_to_all.88 = f32[8,32,65]{2,1,0:T(8,128)S(1)} all-to-all(f32[8,32,65]{2,1,0:T(8,128)S(1)} %copy.29), channel_id=1, replica_groups=mesh['blk_0'=4,'blk_1'=8,'sub_0'=4,'sub_1'=2] {'sub_0','sub_1'}, dimensions={0} | all-to-all | bytes 133120 | tf_op jit(solution)/shard_map/all_to_all | solution.py:50
  598.4 13.3 %all_to_all.89 = f32[32,1,65]{2,1,0:T(1,128)S(1)} all-to-all(f32[32,1,65]{2,1,0:T(1,128)S(1)} %bitcast.67), channel_id=1, replica_groups=mesh['blk_0'=4,'blk_1'=8,'sub_0'=4,'sub_1'=2] {'blk_0','blk_1'}, dimensions={0} | all-to-all | bytes 16640 | tf_op jit(solution)/shard_map/all_to_all | solution.py:58
  611.7 11.6 %all_to_all.90 = f32[32,1,65]{2,1,0:T(1,128)S(1)} all-to-all(f32[32,1,65]{2,1,0:T(1,128)S(1)} %broadcast_in_dim.24), channel_id=1, replica_groups=mesh['blk_0'=4,'blk_1'=8,'sub_0'=4,'sub_1'=2] {'blk_0','blk_1'}, dimensions={0} | all-to-all | bytes 16640 | tf_op jit(solution)/shard_map/all_to_all | solution.py:25
  623.3 0.7 broadcast_in_dim.26
  624.0 6.7 %all-to-all-start.14 = ((f32[8,32,65]{2,1,0:T(8,128)}), f32[8,32,65]{2,1,0:T(8,128)S(1)}, u32[]{:S(2)}, u32[]{:S(2)}) async-start(f32[8,32,65]{2,1,0:T(8,128)} %broadcast_in_dim.26), calls=%async_computation.14 | async-start | bytes 262144 | tf_op jit(solution)/shard_map/all_to_all | solution.py:25
  630.7 1.1 fusion.34
  631.8 4.2 all-to-all-done.14
  636.0 0.1 copy.30
  636.1 0.2 slice.12
  636.3 0.2 reshape_reshape.15
  636.5 0.6 slice.25
  637.1 0.5 slice.26
  (28 shorter events, 0.2 us)
Async XLA Ops:
  0.6 13.3 %copy-start = (f32[512,128]{1,0:T(8,128)S(1)}, f32[512,128]{1,0:T(8,128)}, u32[]{:S(2)}) copy-start(f32[512,128]{1,0:T(8,128)} %param.8) | copy-start | bytes 786436
  2.1 20.5 %all-to-all-start = ((s32[32,1,2]{2,1,0:T(1,128)}), s32[32,1,2]{2,1,0:T(1,128)S(1)}, u32[]{:S(2)}, u32[]{:S(2)}) async-start(s32[32,1,2]{2,1,0:T(1,128)} %bitcast), calls=%async_computation | async-start | bytes 32768 | tf_op jit(solution)/shard_map/all_to_all | solution.py:98
  23.5 16.7 %all-to-all-start.1 = ((f32[4,512,128]{2,1,0:T(8,128)}), f32[4,512,128]{2,1,0:T(8,128)S(1)}, u32[]{:S(2)}, u32[]{:S(2)}) async-start(f32[4,512,128]{2,1,0:T(8,128)} %broadcast_in_dim.18), calls=%async_computation.1 | async-start | bytes 2097152 | tf_op jit(solution)/shard_map/all_to_all | solution.py:25
  51.9 5.0 copy-start.1
  51.9 5.8 copy-start.6
  51.9 97.5 %all-to-all-start.4 = ((f32[32,2,128,128]{3,2,1,0:T(8,128)}), f32[32,2,128,128]{3,2,1,0:T(8,128)}, u32[]{:S(2)}, u32[]{:S(2)}) async-start(f32[32,2,128,128]{3,2,1,0:T(8,128)} %bitcast.57), calls=%async_computation.4 | async-start | bytes 8388608 | tf_op jit(solution)/shard_map/all_to_all | solution.py:116
  149.4 103.9 %all-to-all-start.3 = ((f32[32,2,128,128]{3,2,1,0:T(8,128)}), f32[32,2,128,128]{3,2,1,0:T(8,128)}, u32[]{:S(2)}, u32[]{:S(2)}) async-start(f32[32,2,128,128]{3,2,1,0:T(8,128)} %bitcast.58), calls=%async_computation.3 | async-start | bytes 8388608 | tf_op jit(solution)/shard_map/all_to_all | solution.py:109
  253.3 6.2 copy-start.2
  265.6 33.5 %copy-start.3 = (f32[512,128]{1,0:T(8,128)S(1)}, f32[512,128]{1,0:T(8,128)}, u32[]{:S(2)}) copy-start(f32[512,128]{1,0:T(8,128)} %param.15) | copy-start | bytes 786436
  265.6 33.5 %copy-start.5 = (f32[128]{0:T(128)S(1)}, f32[128]{0:T(128)}, u32[]{:S(2)}) copy-start(f32[128]{0:T(128)} %param.10) | copy-start | bytes 1540
  338.9 98.8 %all-to-all-start.8 = ((f32[32,2,128,128]{3,2,1,0:T(8,128)}), f32[32,2,128,128]{3,2,1,0:T(8,128)}, u32[]{:S(2)}, u32[]{:S(2)}) async-start(f32[32,2,128,128]{3,2,1,0:T(8,128)} %bitcast.61), calls=%async_computation.8 | async-start | bytes 8388608 | tf_op jit(solution)/shard_map/all_to_all | solution.py:109
  437.6 100.8 %all-to-all-start.9 = ((f32[32,2,128,128]{3,2,1,0:T(8,128)}), f32[32,2,128,128]{3,2,1,0:T(8,128)}, u32[]{:S(2)}, u32[]{:S(2)}) async-start(f32[32,2,128,128]{3,2,1,0:T(8,128)} %bitcast.59), calls=%async_computation.9 | async-start | bytes 8388608 | tf_op jit(solution)/shard_map/all_to_all | solution.py:116
  553.4 77.4 %copy-start.4 = (f32[128,128]{1,0:T(8,128)S(1)}, f32[128,128]{1,0:T(8,128)}, u32[]{:S(2)}) copy-start(f32[128,128]{1,0:T(8,128)} %param.9) | copy-start | bytes 196612
  553.4 35.3 %all-to-all-start.10 = ((f32[8,512,128]{2,1,0:T(8,128)}), f32[8,512,128]{2,1,0:T(8,128)S(1)}, u32[]{:S(2)}, u32[]{:S(2)}) async-start(f32[8,512,128]{2,1,0:T(8,128)} %reshape_reshape.13), calls=%async_computation.10 | async-start | bytes 4194304 | tf_op jit(solution)/shard_map/all_to_all | solution.py:50
  624.0 12.0 %all-to-all-start.14 = ((f32[8,32,65]{2,1,0:T(8,128)}), f32[8,32,65]{2,1,0:T(8,128)S(1)}, u32[]{:S(2)}, u32[]{:S(2)}) async-start(f32[8,32,65]{2,1,0:T(8,128)} %broadcast_in_dim.26), calls=%async_computation.14 | async-start | bytes 262144 | tf_op jit(solution)/shard_map/all_to_all | solution.py:25
where the time goes:
time: 646 us; the launch traced here: 638 us
  waiting for transfers between devices  387 us (60%)
  blocking collectives  98.9 us (15%)
  matrix products  66.4 us (10%)
  starting transfers between devices  59.8 us (9%)
  local copies, waits for them, and re-layouts  21.8 us (3%)
    all_to_all x2, waiting for transfers between devices, aggregate(): lax.all_to_all(pushed.reshape(block_count, CAP, BS, width), BLK, split_ax...  174 us
    all_to_all x2, waiting for transfers between devices, aggregate(): lax.all_to_all(answer, BLK, split_axis=0, concat_axis=0, tiled=True)  163 us
    all_to_all x4, blocking collectives, copy_for_each(): lax.all_to_all(jnp.broadcast_to(value[None], (peers, *value.shape)), axis...  43.7 us
    all_to_all x2, blocking collectives, summed_on_arrival(): lax.all_to_all(cut_along(value, dim, peers), axis, 0, 0, tiled=True)  41.9 us
    all_to_all x1, waiting for transfers between devices, summed_on_arrival(): lax.all_to_all(cut_along(value, dim, peers), axis, 0, 0, tiled=True)  26.2 us
    dot_general x2, matrix products, aggregate(): jnp.einsum('kji,kjf->kif', masked_tiles, gathered[row_local], precision=l...  24.7 us
    dot_general x2, matrix products, aggregate(): jnp.einsum('kij,kjf->kif', masked_tiles, fetched, precision=lax.Precision...  16.7 us
    all_to_all x2, waiting for transfers between devices, copy_for_each(): lax.all_to_all(jnp.broadcast_to(value[None], (peers, *value.shape)), axis...  16.6 us
  transfers between devices with their start and end apart: 8, of which 8 were waited for; matrix products, arithmetic and copies ran while one was open for 6% of the time, Pallas kernels for 0%

commit v1 on v0

v1 whole, which is shorter than its diff:
```python
import functools
import math

import jax
import jax.numpy as jnp
from jax import lax
from jax.experimental import pallas as pl
from jax.experimental.pallas import tpu as pltpu
from jax.sharding import Mesh
from jax.sharding import PartitionSpec as P

CAP = 2
MESH = pl.DeviceIdType.MESH
AX, AZ, AY, AC = "blk_0", "blk_1", "sub_0", "sub_1"
ALL = (AX, AZ, AY, AC)
BLK = (AX, AZ)
F32 = jnp.float32


def copy_to(src, dst, sends, recvs, at, where):
    return pltpu.make_async_remote_copy(
        src_ref=src,
        dst_ref=dst,
        send_sem=sends.at[at],
        recv_sem=recvs.at[at],
        device_id=where,
        device_id_type=MESH,
    )


def greet(places):
    barrier = pltpu.get_barrier_semaphore()
    for place in places:
        pl.semaphore_signal(barrier, inc=1, device_id=place, device_id_type=MESH)
    pl.semaphore_wait(barrier, len(places))


def visiting_order(count):
    order = [0]
    for step in range(1, count // 2 + 1):
        order.append(step)
        if count - step > count // 2:
            order.append(count - step)
    return order


def pull_kernel(sizes, wanted, own_ref, out_ref, *scratch):
    nx, nz, ny = sizes
    groups = scratch[:nz]
    picks, relays, kept = scratch[nz : nz + 3]
    zs, zr, ys, yr, cs, cr, xs, xr, ls = scratch[nz + 3 :]
    own = own_ref.shape[0]
    half = own // 2
    x, z, y, c = (lax.axis_index(a) for a in (AX, AZ, AY, AC))
    east, west = {AX: (x + 1) % nx}, {AX: (x + nx - 1) % nx}
    up, down = {AZ: (z + 1) % nz}, {AZ: (z + nz - 1) % nz}
    fore, back = {AY: (y + 1) % ny}, {AY: (y + ny - 1) % ny}
    mate = {AC: 1 - c}

    def part(j, away, core, first=0, count=own):
        line = (y + away + ny) % ny
        return groups[j].at[pl.ds((line * 2 + core) * own + first, count)]

    def mine(j):
        return own_ref if j == 0 else part(j, 0, c)

    def along_z(j):
        if j <= nz // 2:
            return copy_to(mine(j - 1), part(j, 0, c), zs, zr, j, up)
        return copy_to(mine((j + 1) % nz), part(j, 0, c), zs, zr, j, down)

    def along_y(j, kind):
        if kind == 0:
            return copy_to(mine(j), part(j, 0, c), ys, yr, (j, 0), fore)
        if kind == 1:
            return copy_to(mine(j), part(j, 0, c), ys, yr, (j, 1), back)
        if kind == 2:
            piece = part(j, -1, c, 0, half)
            return copy_to(piece, piece, ys, yr, (j, 2), fore)
        piece = part(j, 1, c, half, half)
        return copy_to(piece, piece, ys, yr, (j, 3), back)

    def landed_y(j, kind):
        if kind == 0:
            piece = part(j, -1, c)
        elif kind == 1:
            piece = part(j, 1, c)
        elif kind == 2:
            piece = part(j, 2, c, 0, half)
        else:
            piece = part(j, 2, c, half, half)
        copy_to(piece, piece, ys, yr, (j, kind), fore).wait_recv()

    def to_mate(j, kind):
        away = (0, -1, 1, 2)[kind]
        source = mine(j) if kind == 0 else part(j, away, c)
        return copy_to(source, part(j, away, c), cs, cr, (j, kind), mate)

    def landed_mate(j, kind):
        piece = part(j, (0, -1, 1, 2)[kind], 1 - c)
        copy_to(piece, piece, cs, cr, (j, kind), mate).wait_recv()

    def far(j):
        return (z + nz - j) % nz

    def line(away, j):
        return ((x + away + nx) % nx) * nz + far(j)

    def along_x(j, kind):
        if kind == 0:
            return copy_to(picks.at[j, pl.ds(0, 4)], out_ref.at[line(0, j)], xs, xr, (j, 0), east)
        if kind == 1:
            return copy_to(picks.at[j, pl.ds(4, 4)], out_ref.at[line(0, j)], xs, xr, (j, 1), west)
        if kind == 2:
            return copy_to(picks.at[j, pl.ds(8, 2)], relays.at[j, 0], xs, xr, (j, 2), east)
        if kind == 3:
            return copy_to(picks.at[j, pl.ds(10, 2)], relays.at[j, 1], xs, xr, (j, 3), west)
        if kind == 4:
            return copy_to(relays.at[j, 0], out_ref.at[line(-1, j), pl.ds(0, 2)], xs, xr, (j, 4), east)
        return copy_to(relays.at[j, 1], out_ref.at[line(1, j), pl.ds(2, 2)], xs, xr, (j, 5), west)

    def landed_x(j, kind):
        if kind == 0:
            piece = out_ref.at[line(-1, j)]
        elif kind == 1:
            piece = out_ref.at[line(1, j)]
        elif kind in (2, 3):
            piece = relays.at[j, kind - 2]
        elif kind == 4:
            piece = out_ref.at[line(2, j), pl.ds(0, 2)]
        else:
            piece = out_ref.at[line(2, j), pl.ds(2, 2)]
        copy_to(piece, piece, xs, xr, (j, kind), east).wait_recv()

    def keep(j):
        return pltpu.make_async_copy(kept.at[j], out_ref.at[line(0, j)], ls.at[j])

    order = visiting_order(nz)

    def spread(j):
        if j:
            along_z(j).wait_recv()
        if j == 0:
            along_z(1).start()
            if nz - 1 > nz // 2:
                along_z(nz - 1).start()
        elif j < nz // 2:
            along_z(j + 1).start()
        elif j > nz // 2 + 1:
            along_z(j - 1).start()
        along_y(j, 0).start()
        along_y(j, 1).start()
        to_mate(j, 0).start()

    def pass_on(j):
        landed_y(j, 0)
        along_y(j, 2).start()
        landed_y(j, 1)
        along_y(j, 3).start()
        to_mate(j, 1).start()
        to_mate(j, 2).start()
        landed_y(j, 2)
        landed_y(j, 3)
        to_mate(j, 3).start()

    def pick(j):
        for kind in range(4):
            landed_mate(j, kind)

        def asked(away, slot):
            return wanted[(((x + away) % nx) * nz + far(j)) * 4 + slot]

        def one(slot, carry):
            picks[j, slot] = groups[j][asked(1, slot)]
            picks[j, 4 + slot] = groups[j][asked(nx - 1, slot)]
            picks[j, 8 + slot] = groups[j][asked(2, slot)]
            kept[j, slot] = groups[j][asked(0, slot)]
            return carry

        lax.fori_loop(0, 4, one, 0)

    def answer(j):
        for kind in (2, 3, 0, 1):
            along_x(j, kind).start()
        keep(j).start()

    def relay(j):
        for kind in (2, 3):
            landed_x(j, kind)
            along_x(j, kind + 2).start()

    greet((east, west, up, down, fore, back, mate))
    spread(order[0])
    groups[0][pl.ds((y * 2 + c) * own, own)] = own_ref[...]
    spread(order[1])
    for n, j in enumerate(order):
        pass_on(j)
        pick(j)
        if n + 2 < nz:
            spread(order[n + 2])
        if n:
            relay(order[n - 1])
        answer(j)
    relay(order[-1])
    for j in order:
        for kind in (0, 1, 4, 5):
            landed_x(j, kind)
        keep(j).wait()
        if j:
            along_z(j).wait_send()
        for kind in range(4):
            along_y(j, kind).wait_send()
            to_mate(j, kind).wait_send()
        for kind in range(6):
            along_x(j, kind).wait_send()


def pull(sizes, wanted, value):
    nx, nz, ny = sizes
    own, rows, width = value.shape
    block = (rows, width)
    dma = pltpu.SemaphoreType.DMA
    return pl.pallas_call(
        functools.partial(pull_kernel, sizes),
        out_shape=jax.ShapeDtypeStruct((nx * nz, 4, *block), F32),
        in_specs=[
            pl.BlockSpec(memory_space=pltpu.SMEM),
            pl.BlockSpec(memory_space=pltpu.VMEM),
        ],
        out_specs=pl.BlockSpec(memory_space=pl.ANY),
        scratch_shapes=[pltpu.VMEM((ny * 2 * own, *block), F32) for _ in range(nz)]
        + [
            pltpu.VMEM((nz, 12, *block), F32),
            pltpu.VMEM((nz, 2, 2, *block), F32),
            pltpu.VMEM((nz, 4, *block), F32),
            dma((nz,)),
            dma((nz,)),
            dma((nz, 4)),
            dma((nz, 4)),
            dma((nz, 4)),
            dma((nz, 4)),
            dma((nz, 6)),
            dma((nz, 6)),
            dma((nz,)),
        ],
        compiler_params=pltpu.CompilerParams(
            collective_id=0, has_side_effects=True, vmem_limit_bytes=48 * 2**20
        ),
        cost_estimate=pl.CostEstimate(
            flops=20_000_000_000, bytes_accessed=17_000_000, transcendentals=0
        ),
        name="pull",
    )(wanted, value)


def scatter_kernel(ny, sums, out_ref, mated, total, early, late, cs, cr, ys, yr):
    own = out_ref.shape[0]
    half = own // 2
    y, c = lax.axis_index(AY), lax.axis_index(AC)
    fore, back, mate = {AY: (y + 1) % ny}, {AY: (y + ny - 1) % ny}, {AC: 1 - c}

    def at(away, core):
        return pl.ds((((y + away) % ny) * 2 + core) * own, own)

    def over(k):
        return copy_to(sums.at[at(k, 1 - c)], mated.at[k], cs, cr, k, mate)

    early_fore = copy_to(total.at[2, pl.ds(0, half)], early.at[0], ys, yr, 0, fore)
    early_back = copy_to(total.at[2, pl.ds(half, half)], early.at[1], ys, yr, 1, back)
    late_fore = copy_to(total.at[1], late.at[0], ys, yr, 2, fore)
    late_back = copy_to(total.at[3], late.at[1], ys, yr, 3, back)
    greet((fore, back, mate))
    for k in (2, 1, 3, 0):
        over(k).start()
    for k in (2, 1, 3, 0):
        over(k).wait_recv()
        total[k] = sums[at(k, c)] + mated[k]
        if k == 1:
            early_fore.start()
            early_back.start()
    early_fore.wait_recv()
    total[1, pl.ds(0, half)] = total[1, pl.ds(0, half)] + early[0]
    early_back.wait_recv()
    total[3, pl.ds(half, half)] = total[3, pl.ds(half, half)] + early[1]
    late_fore.start()
    late_back.start()
    late_fore.wait_recv()
    late_back.wait_recv()
    out_ref[...] = total[0] + late[0] + late[1]
    for k in range(4):
        over(k).wait_send()
    for copy in (early_fore, early_back, late_fore, late_back):
        copy.wait_send()


def scatter(ny, sums):
    count, rows, width = sums.shape
    own = count // (2 * ny)
    dma = pltpu.SemaphoreType.DMA
    piece = (own, rows, width)
    return pl.pallas_call(
        functools.partial(scatter_kernel, ny),
        out_shape=jax.ShapeDtypeStruct(piece, F32),
        in_specs=[pl.BlockSpec(memory_space=pltpu.VMEM)],
        out_specs=pl.BlockSpec(memory_space=pltpu.VMEM),
        scratch_shapes=[
            pltpu.VMEM((4, *piece), F32),
            pltpu.VMEM((4, *piece), F32),
            pltpu.VMEM((2, own // 2, rows, width), F32),
            pltpu.VMEM((2, *piece), F32),
            dma((4,)),
            dma((4,)),
            dma((4,)),
            dma((4,)),
        ],
        compiler_params=pltpu.CompilerParams(
            collective_id=1, has_side_effects=True, vmem_limit_bytes=16 * 2**20
        ),
        cost_estimate=pl.CostEstimate(
            flops=2_000_000_000, bytes_accessed=2_000_000, transcendentals=0
        ),
        name="scatter",
    )(sums)


def halves(value):
    high = value.astype(jnp.bfloat16)
    return high, (value - high.astype(F32)).astype(jnp.bfloat16)


def product(tile, value, flipped):
    dims = (((0 if flipped else 1,), (0,)), ((), ()))
    tile_high, tile_low = halves(tile)
    high, low = halves(value)

    def dot(a, b):
        return lax.dot_general(a, b, dims, preferred_element_type=F32)

    return dot(tile_high, high) + (dot(tile_high, low) + dot(tile_low, high))


def apply_kernel(step, target, alive, near, moved, values, sums):
    first = pl.program_id(0) * step

    @pl.when(first == 0)
    def _():
        sums[...] = jnp.zeros_like(sums)

    for g in range(step):
        for slot in range(4):
            place = (first + g) * 4 + slot
            block = (near if slot < 2 else moved)[g, slot % 2]

            @pl.when(alive[place] > 0)
            def _(block=block, place=place, g=g, slot=slot):
                sums[target[place]] += product(block, values[g, slot], slot >= 2)


def apply(group_size, target, alive, near, moved, values):
    count, _, rows, width = values.shape
    step = 2
    tiles = pl.BlockSpec((step, 2, rows, rows), lambda n, *_: (n, 0, 0, 0))
    return pl.pallas_call(
        functools.partial(apply_kernel, step),
        out_shape=jax.ShapeDtypeStruct((group_size, rows, width), F32),
        grid_spec=pltpu.PrefetchScalarGridSpec(
            num_scalar_prefetch=2,
            grid=(count // step,),
            in_specs=[
                tiles,
                tiles,
                pl.BlockSpec((step, 4, rows, width), lambda n, *_: (n, 0, 0, 0)),
            ],
            out_specs=pl.BlockSpec((group_size, rows, width), lambda n, *_: (0, 0, 0)),
        ),
        compiler_params=pltpu.CompilerParams(vmem_limit_bytes=24 * 2**20),
        cost_estimate=pl.CostEstimate(
            flops=count * 4 * 6 * rows * rows * width,
            bytes_accessed=19_000_000,
            transcendentals=0,
        ),
        name="apply",
    )(target, alive, near, moved, values)


def exchanged(value, axis):
    return lax.all_to_all(value, axis, 0, 0, tiled=True)


def far_sum(pieces, axis):
    return exchanged(pieces, axis).sum(axis=0)


def for_each(value, axis):
    peers = lax.axis_size(axis)
    return exchanged(jnp.broadcast_to(value[None], (peers, *value.shape)), axis)


def param_sum(vector):
    blocks, subs = lax.axis_size(BLK), lax.axis_size((AY, AC))
    spare = -vector.shape[0] % (blocks * subs)
    padded = jnp.concatenate([vector, jnp.zeros((spare,), F32)]).reshape(blocks, subs, -1)
    near = far_sum(padded.swapaxes(0, 1), (AY, AC))
    done = far_sum(near, BLK)
    line = for_each(done, BLK)
    whole = for_each(line, (AY, AC))
    return whole.swapaxes(0, 1).reshape(-1)[: vector.shape[0]]


def body(features, weight, bias, adj_tiles, tile_rows, tile_cols, tile_counts, cotangent):
    nx, nz, ny = (lax.axis_size(a) for a in (AX, AZ, AY))
    sizes = (nx, nz, ny)
    blocks = nx * nz
    rows, width = adj_tiles.shape[1], features.shape[1]
    own = features.shape[0] // rows
    group_size = own * ny * 2
    group = lax.axis_index(BLK)
    scale = 1.0 / math.sqrt(features.shape[0] * blocks * ny * 2)
    slots = jnp.arange(blocks * CAP, dtype=jnp.int32)
    alive = (slots % CAP < tile_counts[slots // CAP]).astype(jnp.int32)
    row_local = tile_rows - group * group_size
    col_local = tile_cols - slots // CAP * group_size
    near = adj_tiles.reshape(blocks, CAP, rows, rows)
    moved = exchanged(near, BLK)

    by_group = (blocks, CAP)
    told = exchanged(
        jnp.concatenate([col_local.reshape(by_group), alive.reshape(by_group)], axis=1), BLK
    )
    direct = exchanged(col_local.reshape(nx, nz, CAP), AX)
    turned = exchanged(row_local.reshape(nx, nz, CAP).swapaxes(0, 1), AZ).swapaxes(0, 1)
    wanted = jnp.concatenate([direct, turned], axis=2).reshape(-1)
    target = jnp.concatenate([row_local.reshape(by_group), told[:, :CAP]], axis=1).reshape(-1)
    live = jnp.concatenate([alive.reshape(by_group), told[:, CAP:]], axis=1).reshape(-1)

    def aggregate(value):
        fetched = pull(sizes, wanted, value.reshape(own, rows, width))
        sums = apply(group_size, target, live, near, moved, fetched)
        return scatter(ny, sums).reshape(value.shape)

    dot = functools.partial(jnp.dot, precision=lax.Precision.HIGHEST)
    spread = aggregate(features)
    pre = dot(spread, weight) + bias
    sigma = jax.nn.sigmoid(pre)
    activation = pre * sigma
    grad_pre = cotangent * sigma * (1.0 + pre * (1.0 - sigma))
    vector = jnp.concatenate(
        [(dot(spread.T, grad_pre) * scale).reshape(-1), jnp.sum(grad_pre, axis=0) * scale]
    )
    params = param_sum(vector)
    grad_mixed = aggregate(grad_pre)
    grad_features = dot(grad_mixed, weight.T)
    grad_weight = params[: weight.size].reshape(weight.shape)
    return (activation, grad_features, grad_weight, params[weight.size :])


def solution(mesh):
    finer = Mesh(mesh.devices.reshape(4, 8, 4, 2), ALL)
    return jax.shard_map(
        body,
        mesh=finer,
        in_specs=(
            P(ALL, None),
            P(),
            P(),
            P(ALL, None, None),
            P(ALL),
            P(ALL),
            P(ALL),
            P(ALL, None),
        ),
        out_specs=(P(ALL, None), P(ALL, None), P(), P()),
        check_vma=False,
    )
```

time: 646 us -> 508 us (0.79)
  Pallas kernels: 0 us -> 414 us
  waiting for transfers between devices: 387 us -> 11.5 us
  blocking collectives: 98.9 us -> 12.6 us
  matrix products: 66.4 us -> 2.81 us
  starting transfers between devices: 59.8 us -> 42.1 us
    pallas_call x0 -> x6, Pallas kernels: none -> 414 us  [the longest x2 340 us: pull(): pl.pallas_call(functools.partial(pull_kernel, sizes), out_shape=jax.Shape...]
    all_to_all x8 -> x7, waiting for transfers between devices: 387 us -> 11.5 us  [exchanged(): return lax.all_to_all(value, axis, 0, 0, tiled=True)]
    all_to_all x7 -> x1, blocking collectives: 98.9 us -> 12.6 us  [exchanged(): return lax.all_to_all(value, axis, 0, 0, tiled=True)]
    dot_general x11 -> x3, matrix products: 66.4 us -> 2.81 us  [the longest x1 1.15 us: body(): pre = dot(spread, weight) + bias]
    all_to_all x8 -> x7, starting transfers between devices: 59.8 us -> 42.1 us  [exchanged(): return lax.all_to_all(value, axis, 0, 0, tiled=True)]
    unnamed x14 -> x18, local copies, waits for them, and re-layouts: 0.03 us -> 11.3 us
    gather x5 -> x2, local copies, waits for them, and re-layouts: 11.8 us -> 1.53 us  [body(): alive = (slots % CAP < tile_counts[slots // CAP]).astype(jnp.int32)]
  transfers between devices with their start and end apart: 8 -> 7, of which waited for: 8 -> 3; matrix products, arithmetic and copies ran while one was open for 6% -> 1% of each run, Pallas kernels for 0% -> 75%
where the time goes in v1:
time: 508 us; the launch traced here: 506 us
  Pallas kernels  414 us (81%)
  starting transfers between devices  42.1 us (8%)
  local copies, waits for them, and re-layouts  19.3 us (4%)
  blocking collectives  12.6 us (2%)
  waiting for transfers between devices  11.5 us (2%)
    pallas_call x2, Pallas kernels, pull(): pl.pallas_call(functools.partial(pull_kernel, sizes), out_shape=jax.Shape...  340 us
    all_to_all x7, starting transfers between devices, exchanged(): return lax.all_to_all(value, axis, 0, 0, tiled=True)  42.1 us
    pallas_call x2, Pallas kernels, apply(): pl.pallas_call(functools.partial(apply_kernel, step), out_shape=jax.Shape...  38.4 us
    pallas_call x2, Pallas kernels, scatter(): pl.pallas_call(functools.partial(scatter_kernel, ny), out_shape=jax.Shape...  35.4 us
    all_to_all x1, blocking collectives, exchanged(): return lax.all_to_all(value, axis, 0, 0, tiled=True)  12.6 us
    all_to_all x7, waiting for transfers between devices, exchanged(): return lax.all_to_all(value, axis, 0, 0, tiled=True)  11.5 us
    unnamed x18, local copies, waits for them, and re-layouts  11.3 us
  transfers between devices with their start and end apart: 7, of which 3 were waited for; matrix products, arithmetic and copies ran while one was open for 1% of the time, Pallas kernels for 75%

profile of v1, /device:TPU:1, one launch (start us, length us, event | category | flops | bytes accessed | tf_op | source)
XLA Modules:
  0.0 505.7 jit_solution(3015592327683475513)
XLA Ops:
  0.6 0.0 copy-start
  0.6 0.7 fusion.6
  1.3 0.1 reshape.121
  1.4 0.7 copy.51
  2.1 4.8 all-to-all-start.2
  7.0 0.1 reshape.117
  7.1 1.4 gather_fusion
  8.5 0.1 gather.6
  8.7 0.1 copy.46
  8.7 0.1 copy.45
  8.8 0.7 broadcast_subtract_fusion
  9.5 0.1 reshape.122
  9.6 0.7 copy.52
  10.3 0.8 all-to-all-done.2
  11.1 8.2 %all-to-all-start.3 = ((s32[8,4,2]{1,2,0:T(2,128)}), s32[8,4,2]{1,2,0:T(2,128)S(1)}, u32[]{:S(2)}, u32[]{:S(2)}) async-start(s32[8,4,2]{1,2,0:T(2,128)} %copy.52), calls=%async_computation.3 | async-start | bytes 16384 | tf_op jit(solution)/shard_map/all_to_all | solution.py:387
  19.3 0.1 copy.47
  19.4 6.5 %all-to-all-done.3 = s32[8,4,2]{1,2,0:T(2,128)S(1)} async-done(((s32[8,4,2]{1,2,0:T(2,128)}), s32[8,4,2]{1,2,0:T(2,128)S(1)}, u32[]{:S(2)}, u32[]{:S(2)}) %all-to-all-start.3) | async-done | bytes 288 | tf_op jit(solution)/shard_map/all_to_all | solution.py:387
  25.9 12.6 %all_to_all.52 = s32[32,1,4]{2,1,0:T(1,128)S(1)} all-to-all(s32[32,1,4]{2,1,0:T(1,128)S(1)} %copy.47), channel_id=1, replica_groups=mesh['blk_0'=4,'blk_1'=8,'sub_0'=4,'sub_1'=2] {'blk_0','blk_1'}, dimensions={0} | all-to-all | bytes 1024 | tf_op jit(solution)/shard_map/all_to_all | solution.py:387
  38.5 5.0 all-to-all-start.1
  43.5 0.1 reshape.116
  43.6 0.1 copy.53
  43.7 0.1 copy.54
  43.8 0.1 reshape.123.wanted
  43.9 214.1 %pull.2.values = f32[32,4,128,128]{3,2,1,0:T(8,128)} custom-call(s32[128]{0:T(128)S(1)} %reshape.123.wanted, f32[4,128,128]{2,1,0:T(8,128)S(1)} %bitcast.31), custom_call_target="tpu_custom_call" | custom-call | flops 20000000000 | bytes 17000000 | tf_op jit(solution)/shard_map/pull/pallas_call | solution.py:223
  258.0 0.1 copy.48
  258.1 0.1 copy.59
  258.2 0.1 pad_add_fusion.1
  258.2 0.1 reshape.119.alive
  258.3 0.1 copy.58
  258.4 0.1 pad_add_fusion
  258.5 0.1 reshape.118.target
  258.6 0.0 copy-start.1
  258.6 2.2 copy-done.1
  260.8 3.4 copy-done.3
  264.2 19.2 %apply.2.sums = f32[32,128,128]{2,1,0:T(8,128)S(1)} custom-call(s32[128]{0:T(128)S(1)} %reshape.118.target, s32[128]{0:T(128)S(1)} %reshape.119.alive, f32[32,2,128,128]{3,2,1,0:T(8,128)S(1)} %bitcast.25, f32[32,2,128,128]{3,2,1,0:T(8,128)} %all-to-all-done.1.moved, f32[32,4,128,128]{3,2,1,0:T(8,128)S(1)} %copy-done.3), custom_call_target="tpu_custom_call" | custom-call | flops 1610612736 | bytes 19000000 | tf_op jit(solution)/shard_map/apply/pallas_call | solution.py:363
  283.4 0.0 copy-start.6
  283.4 0.0 copy-start.7
  283.4 16.2 %scatter.2 = f32[4,128,128]{2,1,0:T(8,128)S(1)} custom-call(f32[32,128,128]{2,1,0:T(8,128)S(1)} %apply.2.sums), custom_call_target="tpu_custom_call" | custom-call | flops 2000000000 | bytes 2000000 | tf_op jit(solution)/shard_map/scatter/pallas_call | solution.py:301
  299.6 1.1 fusion.8
  300.8 0.6 fusion
  301.4 0.2 reshape.129
  301.6 0.7 copy.55
  302.3 5.3 %all-to-all-start.4 = ((f32[8,32,65]{2,1,0:T(8,128)}), f32[8,32,65]{2,1,0:T(8,128)S(1)}, u32[]{:S(2)}, u32[]{:S(2)}) async-start(f32[8,32,65]{2,1,0:T(8,128)} %copy.55), calls=%async_computation.4 | async-start | bytes 262144 | tf_op jit(solution)/shard_map/all_to_all | solution.py:387
  307.5 126.4 %pull.3.values = f32[32,4,128,128]{3,2,1,0:T(8,128)} custom-call(s32[128]{0:T(128)S(1)} %reshape.123.wanted, f32[4,128,128]{2,1,0:T(8,128)S(1)} %bitcast.27), custom_call_target="tpu_custom_call" | custom-call | flops 20000000000 | bytes 17000000 | tf_op jit(solution)/shard_map/pull/pallas_call | solution.py:223
  433.9 0.0 all-to-all-done.4
  434.0 0.6 reduce_sum.28
  434.6 5.1 %all-to-all-start.5 = ((f32[32,1,65]{2,1,0:T(1,128)}), f32[32,1,65]{2,1,0:T(1,128)S(1)}, u32[]{:S(2)}, u32[]{:S(2)}) async-start(f32[32,1,65]{2,1,0:T(1,128)} %bitcast.12), calls=%async_computation.5 | async-start | bytes 32768 | tf_op jit(solution)/shard_map/all_to_all | solution.py:387
  439.7 0.0 copy-start.2
  439.7 2.2 copy-done.2
  441.9 3.4 copy-done.4
  445.3 19.2 %apply.3.sums = f32[32,128,128]{2,1,0:T(8,128)S(1)} custom-call(s32[128]{0:T(128)S(1)} %reshape.118.target, s32[128]{0:T(128)S(1)} %reshape.119.alive, f32[32,2,128,128]{3,2,1,0:T(8,128)S(1)} %bitcast.26, f32[32,2,128,128]{3,2,1,0:T(8,128)} %all-to-all-done.1.moved, f32[32,4,128,128]{3,2,1,0:T(8,128)S(1)} %copy-done.4), custom_call_target="tpu_custom_call" | custom-call | flops 1610612736 | bytes 19000000 | tf_op jit(solution)/shard_map/apply/pallas_call | solution.py:363
  464.5 0.1 reduce_sum.29
  464.6 0.6 broadcast_in_dim.9
  465.2 10.3 %all-to-all-start.6 = ((f32[32,1,65]{2,1,0:T(1,128)}), f32[32,1,65]{2,1,0:T(1,128)S(1)}, u32[]{:S(2)}, u32[]{:S(2)}) async-start(f32[32,1,65]{2,1,0:T(1,128)} %broadcast_in_dim.9), calls=%async_computation.6 | async-start | bytes 32768 | tf_op jit(solution)/shard_map/all_to_all | solution.py:387
  475.5 19.3 %scatter.3 = f32[4,128,128]{2,1,0:T(8,128)S(1)} custom-call(f32[32,128,128]{2,1,0:T(8,128)S(1)} %apply.3.sums), custom_call_target="tpu_custom_call" | custom-call | flops 2000000000 | bytes 2000000 | tf_op jit(solution)/shard_map/scatter/pallas_call | solution.py:301
  494.8 0.7 broadcast_in_dim.22
  495.5 3.3 all-to-all-start.7
  498.8 1.1 fusion.10
  499.9 4.2 all-to-all-done.7
  504.1 0.1 copy.56
  504.1 0.2 reshape.130
  504.4 0.2 slice.20
  504.6 0.5 slice.26
  505.1 0.6 slice.25
  (19 shorter events, 0.1 us)
Async XLA Ops:
  0.6 299.0 %copy-start = (f32[128,128]{1,0:T(8,128)S(1)}, f32[128,128]{1,0:T(8,128)}, u32[]{:S(2)}) copy-start(f32[128,128]{1,0:T(8,128)} %param.9) | copy-start | bytes 196612
  2.1 9.0 %all-to-all-start.2 = ((s32[4,8,2]{1,2,0:T(2,128)}), s32[4,8,2]{1,2,0:T(2,128)S(1)}, u32[]{:S(2)}, u32[]{:S(2)}) async-start(s32[4,8,2]{1,2,0:T(2,128)} %copy.51), calls=%async_computation.2 | async-start | bytes 8192 | tf_op jit(solution)/shard_map/all_to_all | solution.py:387
  11.1 14.8 %all-to-all-start.3 = ((s32[8,4,2]{1,2,0:T(2,128)}), s32[8,4,2]{1,2,0:T(2,128)S(1)}, u32[]{:S(2)}, u32[]{:S(2)}) async-start(s32[8,4,2]{1,2,0:T(2,128)} %copy.52), calls=%async_computation.3 | async-start | bytes 16384 | tf_op jit(solution)/shard_map/all_to_all | solution.py:387
  38.5 5.4 %copy-start.5 = (f32[512,128]{1,0:T(8,128)S(1)}, f32[512,128]{1,0:T(8,128)}, u32[]{:S(2)}) copy-start(f32[512,128]{1,0:T(8,128)} %param.8) | copy-start | bytes 786436
  38.5 220.2 %all-to-all-start.1 = ((f32[32,2,128,128]{3,2,1,0:T(8,128)}), f32[32,2,128,128]{3,2,1,0:T(8,128)}, u32[]{:S(2)}, u32[]{:S(2)}) async-start(f32[32,2,128,128]{3,2,1,0:T(8,128)} %bitcast.24), calls=%async_computation.1 | async-start | bytes 8388608 | tf_op jit(solution)/shard_map/all_to_all | solution.py:387
  258.6 2.2 copy-start.1
  260.8 3.4 copy-start.3
  283.4 16.2 %copy-start.6 = (f32[512,128]{1,0:T(8,128)S(1)}, f32[512,128]{1,0:T(8,128)}, u32[]{:S(2)}) copy-start(f32[512,128]{1,0:T(8,128)} %param.15) | copy-start | bytes 786436
  283.4 16.2 %copy-start.7 = (f32[128]{0:T(128)S(1)}, f32[128]{0:T(128)}, u32[]{:S(2)}) copy-start(f32[128]{0:T(128)} %param.10) | copy-start | bytes 1540
  302.3 131.7 %all-to-all-start.4 = ((f32[8,32,65]{2,1,0:T(8,128)}), f32[8,32,65]{2,1,0:T(8,128)S(1)}, u32[]{:S(2)}, u32[]{:S(2)}) async-start(f32[8,32,65]{2,1,0:T(8,128)} %copy.55), calls=%async_computation.4 | async-start | bytes 262144 | tf_op jit(solution)/shard_map/all_to_all | solution.py:387
  434.6 29.9 %all-to-all-start.5 = ((f32[32,1,65]{2,1,0:T(1,128)}), f32[32,1,65]{2,1,0:T(1,128)S(1)}, u32[]{:S(2)}, u32[]{:S(2)}) async-start(f32[32,1,65]{2,1,0:T(1,128)} %bitcast.12), calls=%async_computation.5 | async-start | bytes 32768 | tf_op jit(solution)/shard_map/all_to_all | solution.py:387
  439.7 2.2 copy-start.2
  441.9 3.4 copy-start.4
  465.2 29.6 %all-to-all-start.6 = ((f32[32,1,65]{2,1,0:T(1,128)}), f32[32,1,65]{2,1,0:T(1,128)S(1)}, u32[]{:S(2)}, u32[]{:S(2)}) async-start(f32[32,1,65]{2,1,0:T(1,128)} %broadcast_in_dim.9), calls=%async_computation.6 | async-start | bytes 32768 | tf_op jit(solution)/shard_map/all_to_all | solution.py:387
  495.5 8.6 %all-to-all-start.7 = ((f32[8,32,65]{2,1,0:T(8,128)}), f32[8,32,65]{2,1,0:T(8,128)S(1)}, u32[]{:S(2)}, u32[]{:S(2)}) async-start(f32[8,32,65]{2,1,0:T(8,128)} %broadcast_in_dim.22), calls=%async_computation.7 | async-start | bytes 262144 | tf_op jit(solution)/shard_map/all_to_all | solution.py:387

commit v2 on v1

--- a/solution.py
+++ b/solution.py
@@ -44,11 +44,30 @@
     return order
 
 
-def pull_kernel(sizes, wanted, own_ref, out_ref, *scratch):
+def pull_kernel(sizes, first, fuse, *refs):
     nx, nz, ny = sizes
-    groups = scratch[:nz]
-    picks, relays, kept = scratch[nz : nz + 3]
-    zs, zr, ys, yr, cs, cr, xs, xr, ls = scratch[nz + 3 :]
+    refs = list(refs)
+
+    def take(count):
+        taken, refs[:count] = refs[:count], []
+        return taken
+
+    if first:
+        ids_ref, own_ref, near_ref = take(3)
+        out_ref, moved_ref, told_ref = take(3)
+    else:
+        asks, own_ref, near_ref, moved_ref = take(4)
+        (out_ref,) = take(1)
+    groups = take(nz)
+    picks, relays, landing = take(3)
+    zs, zr, ys, yr, cs, cr, xs, xr, ls = take(9)
+    if first or fuse:
+        (moved,) = take(1)
+    if fuse:
+        near, = take(1)
+    if first:
+        passing, tossed, table, asks = take(4)
+        ts, tr, us, ur, js, jr, ms = take(7)
     own = own_ref.shape[0]
     half = own // 2
     x, z, y, c = (lax.axis_index(a) for a in (AX, AZ, AY, AC))
@@ -57,9 +76,9 @@
     fore, back = {AY: (y + 1) % ny}, {AY: (y + ny - 1) % ny}
     mate = {AC: 1 - c}
 
-    def part(j, away, core, first=0, count=own):
+    def part(j, away, core, start=0, count=own):
         line = (y + away + ny) % ny
-        return groups[j].at[pl.ds((line * 2 + core) * own + first, count)]
+        return groups[j].at[pl.ds((line * 2 + core) * own + start, count)]
 
     def mine(j):
         return own_ref if j == 0 else part(j, 0, c)
@@ -103,51 +122,112 @@
     def far(j):
         return (z + nz - j) % nz
 
-    def line(away, j):
-        return ((x + away + nx) % nx) * nz + far(j)
+    def row(away):
+        return (x + away + nx) % nx
 
     def along_x(j, kind):
         if kind == 0:
-            return copy_to(picks.at[j, pl.ds(0, 4)], out_ref.at[line(0, j)], xs, xr, (j, 0), east)
+            return copy_to(picks.at[j, pl.ds(0, 4)], landing.at[x, far(j)], xs, xr, (j, 0), east)
         if kind == 1:
-            return copy_to(picks.at[j, pl.ds(4, 4)], out_ref.at[line(0, j)], xs, xr, (j, 1), west)
+            return copy_to(picks.at[j, pl.ds(4, 4)], landing.at[x, far(j)], xs, xr, (j, 1), west)
         if kind == 2:
             return copy_to(picks.at[j, pl.ds(8, 2)], relays.at[j, 0], xs, xr, (j, 2), east)
         if kind == 3:
             return copy_to(picks.at[j, pl.ds(10, 2)], relays.at[j, 1], xs, xr, (j, 3), west)
         if kind == 4:
-            return copy_to(relays.at[j, 0], out_ref.at[line(-1, j), pl.ds(0, 2)], xs, xr, (j, 4), east)
-        return copy_to(relays.at[j, 1], out_ref.at[line(1, j), pl.ds(2, 2)], xs, xr, (j, 5), west)
+            place = landing.at[row(-1), far(j), pl.ds(0, 2)]
+            return copy_to(relays.at[j, 0], place, xs, xr, (j, 4), east)
+        place = landing.at[row(1), far(j), pl.ds(2, 2)]
+        return copy_to(relays.at[j, 1], place, xs, xr, (j, 5), west)
 
     def landed_x(j, kind):
         if kind == 0:
-            piece = out_ref.at[line(-1, j)]
+            piece = landing.at[row(-1), far(j)]
         elif kind == 1:
-            piece = out_ref.at[line(1, j)]
+            piece = landing.at[row(1), far(j)]
         elif kind in (2, 3):
             piece = relays.at[j, kind - 2]
         elif kind == 4:
-            piece = out_ref.at[line(2, j), pl.ds(0, 2)]
+            piece = landing.at[row(2), far(j), pl.ds(0, 2)]
         else:
-            piece = out_ref.at[line(2, j), pl.ds(2, 2)]
+            piece = landing.at[row(2), far(j), pl.ds(2, 2)]
         copy_to(piece, piece, xs, xr, (j, kind), east).wait_recv()
 
-    def keep(j):
-        return pltpu.make_async_copy(kept.at[j], out_ref.at[line(0, j)], ls.at[j])
+    def tiles_z(d):
+        there = (z + d) % nz
+        return copy_to(near_ref.at[:, there], passing.at[d], ts, tr, d, {AZ: there})
+
+    def tiles_for(j, away):
+        return near_ref.at[row(away), z] if j == 0 else passing.at[j, row(away)]
+
+    def tiles_x(j, kind):
+        if kind == 0:
+            return copy_to(tiles_for(j, 1), moved.at[x, far(j)], us, ur, (j, 0), east)
+        if kind == 1:
+            return copy_to(tiles_for(j, -1), moved.at[x, far(j)], us, ur, (j, 1), west)
+        if kind == 2:
+            return copy_to(tiles_for(j, 2).at[0], tossed.at[j, 0], us, ur, (j, 2), east)
+        if kind == 3:
+            return copy_to(tiles_for(j, 2).at[1], tossed.at[j, 1], us, ur, (j, 3), west)
+        if kind == 4:
+            return copy_to(tossed.at[j, 0], moved.at[row(-1), far(j), 0], us, ur, (j, 4), east)
+        return copy_to(tossed.at[j, 1], moved.at[row(1), far(j), 1], us, ur, (j, 5), west)
+
+    def landed_tiles(j, kind):
+        if kind == 0:
+            piece = moved.at[row(-1), far(j)]
+        elif kind == 1:
+            piece = moved.at[row(1), far(j)]
+        elif kind in (2, 3):
+            piece = tossed.at[j, kind - 2]
+        elif kind == 4:
+            piece = moved.at[row(2), far(j), 0]
+        else:
+            piece = moved.at[row(2), far(j), 1]
+        copy_to(piece, piece, us, ur, (j, kind), east).wait_recv()
+
+    def ids_z(d):
+        return copy_to(ids_ref, table.at[x, z], js, jr, d, {AZ: (z + d) % nz})
+
+    def ids_x(d):
+        return copy_to(table.at[x], table.at[x], js, jr, nz + d, {AX: (x + d) % nx})
+
+    kept_tiles = lambda: pltpu.make_async_copy(near_ref.at[x, z], moved.at[x, z], ls.at[0])
+    all_near = lambda: pltpu.make_async_copy(near_ref, near, ls.at[1])
+    all_moved = lambda: pltpu.make_async_copy(moved_ref, moved, ls.at[2])
+    all_asks = lambda: pltpu.make_async_copy(table, asks, ls.at[3])
+
+    def results(j):
+        return pltpu.make_async_copy(landing.at[:, far(j)], out_ref.at[:, far(j)], ls.at[4 + j])
+
+    def moved_out(j):
+        return pltpu.make_async_copy(moved.at[:, far(j)], moved_ref.at[:, far(j)], ms.at[j])
 
     order = visiting_order(nz)
+    here = {0}
+
+    def await_z(j):
+        if j not in here:
+            here.add(j)
+            along_z(j).wait_recv()
+
+    def z_step(k):
+        for j, step in ((k, 1), (nz - k, -1)):
+            ahead = j + step
+            if k == 0:
+                j, ahead = 0, (1 if step == 1 else nz - 1)
+            if step == 1 and ahead > nz // 2 or step == -1 and ahead <= nz // 2:
+                continue
+            await_z(j)
+            along_z(ahead).start()
+
+    def tile_step(k):
+        if first and k <= nz // 2:
+            for d in sorted({k, nz - k}):
+                tiles_z(d).start()
 
     def spread(j):
-        if j:
-            along_z(j).wait_recv()
-        if j == 0:
-            along_z(1).start()
-            if nz - 1 > nz // 2:
-                along_z(nz - 1).start()
-        elif j < nz // 2:
-            along_z(j + 1).start()
-        elif j > nz // 2 + 1:
-            along_z(j - 1).start()
+        await_z(j)
         along_y(j, 0).start()
         along_y(j, 1).start()
         to_mate(j, 0).start()
@@ -167,45 +247,122 @@
         for kind in range(4):
             landed_mate(j, kind)
 
-        def asked(away, slot):
-            return wanted[(((x + away) % nx) * nz + far(j)) * 4 + slot]
+        def asked(away, slot, late):
+            line = row(away)
+            if late:
+                return asks[x, far(j), 0, (line * nz + z) * CAP + slot]
+            return asks[line, z, 0, nx * nz * CAP + (x * nz + far(j)) * CAP + slot]
 
         def one(slot, carry):
-            picks[j, slot] = groups[j][asked(1, slot)]
-            picks[j, 4 + slot] = groups[j][asked(nx - 1, slot)]
-            picks[j, 8 + slot] = groups[j][asked(2, slot)]
-            kept[j, slot] = groups[j][asked(0, slot)]
+            for late in range(2):
+                place = late * CAP + slot
+                picks[j, place] = groups[j][asked(1, slot, late)]
+                picks[j, 4 + place] = groups[j][asked(-1, slot, late)]
+                picks[j, 8 + place] = groups[j][asked(2, slot, late)]
+                landing[x, far(j), place] = groups[j][asked(0, slot, late)]
             return carry
 
-        lax.fori_loop(0, 4, one, 0)
+        lax.fori_loop(0, CAP, one, 0)
 
     def answer(j):
         for kind in (2, 3, 0, 1):
             along_x(j, kind).start()
-        keep(j).start()
+        if first:
+            if j:
+                tiles_z(j).wait_recv()
+                moved[x, far(j)] = passing[j, x]
+            for kind in (2, 3, 0, 1):
+                tiles_x(j, kind).start()
 
     def relay(j):
         for kind in (2, 3):
             landed_x(j, kind)
             along_x(j, kind + 2).start()
-
-    greet((east, west, up, down, fore, back, mate))
-    spread(order[0])
+        if first:
+            for kind in (2, 3):
+                landed_tiles(j, kind)
+                tiles_x(j, kind + 2).start()
+
+    def finish(j):
+        for kind in (0, 1, 4, 5):
+            landed_x(j, kind)
+            if first:
+                landed_tiles(j, kind)
+        if fuse:
+
+            def one(line, carry):
+                for slot in range(CAP):
+                    value = landing[line, far(j), slot]
+                    landing[line, far(j), slot] = product(near[line, far(j), slot], value, False)
+                    value = landing[line, far(j), CAP + slot]
+                    tile = moved[line, far(j), slot]
+                    landing[line, far(j), CAP + slot] = product(tile, value, True)
+                return carry
+
+            lax.fori_loop(0, nx, one, 0)
+        results(j).start()
+        if first:
+            moved_out(j).start()
+
+    places = [east, west, up, down, fore, back, mate]
+    if first:
+        places += [{AX: (x + 2) % nx}] + [{AZ: (z + d) % nz} for d in range(2, nz - 1)]
+    greet(places)
+    if first:
+        for d in range(1, nz):
+            ids_z(d).start()
+    z_step(0)
+    spread(0)
+    if first:
+        kept_tiles().start()
+        table[x, z] = ids_ref[...]
+    elif fuse:
+        all_moved().start()
+    if fuse:
+        all_near().start()
     groups[0][pl.ds((y * 2 + c) * own, own)] = own_ref[...]
     spread(order[1])
+    z_step(1)
+    if first:
+        for d in range(1, nz):
+            copy_to(table.at[x, far(d)], table.at[x, far(d)], js, jr, d, up).wait_recv()
+        for d in range(1, nx):
+            ids_x(d).start()
     for n, j in enumerate(order):
         pass_on(j)
+        if n == 0:
+            if first:
+                kept_tiles().wait()
+                for d in range(1, nx):
+                    copy_to(table.at[row(-d)], table.at[row(-d)], js, jr, nz + d, east).wait_recv()
+                all_asks().start()
+                all_asks().wait()
+            elif fuse:
+                all_moved().wait()
+            if fuse:
+                all_near().wait()
         pick(j)
         if n + 2 < nz:
             spread(order[n + 2])
+        if n + 2 < nz // 2:
+            z_step(n + 2)
+        if n == 2:
+            for k in range(3, nz // 2 + 1):
+                tile_step(k)
+        elif n < 2:
+            tile_step(n + 1)
         if n:
             relay(order[n - 1])
         answer(j)
+        if n > 1:
+            finish(order[n - 2])
     relay(order[-1])
+    finish(order[-2])
+    finish(order[-1])
+    if first:
+        told_ref[...] = table[...]
     for j in order:
-        for kind in (0, 1, 4, 5):
-            landed_x(j, kind)
-        keep(j).wait()
+        results(j).wait()
         if j:
             along_z(j).wait_send()
         for kind in range(4):
@@ -213,44 +370,90 @@
             to_mate(j, kind).wait_send()
         for kind in range(6):
             along_x(j, kind).wait_send()
-
-
-def pull(sizes, wanted, value):
+        if first:
+            moved_out(j).wait()
+            for kind in range(6):
+                tiles_x(j, kind).wait_send()
+            if j:
+                tiles_z(j).wait_send()
+                ids_z(j).wait_send()
+    if first:
+        for d in range(1, nx):
+            ids_x(d).wait_send()
+
+
+FUSE = False
+
+
+def pull(sizes, asks, value, near, moved=None):
     nx, nz, ny = sizes
+    first = moved is None
     own, rows, width = value.shape
     block = (rows, width)
     dma = pltpu.SemaphoreType.DMA
-    return pl.pallas_call(
-        functools.partial(pull_kernel, sizes),
-        out_shape=jax.ShapeDtypeStruct((nx * nz, 4, *block), F32),
-        in_specs=[
-            pl.BlockSpec(memory_space=pltpu.SMEM),
-            pl.BlockSpec(memory_space=pltpu.VMEM),
-        ],
-        out_specs=pl.BlockSpec(memory_space=pl.ANY),
-        scratch_shapes=[pltpu.VMEM((ny * 2 * own, *block), F32) for _ in range(nz)]
-        + [
-            pltpu.VMEM((nz, 12, *block), F32),
-            pltpu.VMEM((nz, 2, 2, *block), F32),
-            pltpu.VMEM((nz, 4, *block), F32),
+    tiles = (nx, nz, CAP, rows, rows)
+    values = (nx, nz, 2 * CAP, *block)
+    anywhere, vmem = pl.BlockSpec(memory_space=pl.ANY), pl.BlockSpec(memory_space=pltpu.VMEM)
+    smem = pl.BlockSpec(memory_space=pltpu.SMEM)
+    out_shape = [jax.ShapeDtypeStruct(values, F32)]
+    out_specs = [anywhere]
+    in_specs = [smem, vmem, anywhere, anywhere]
+    scratch = [pltpu.VMEM((ny * 2 * own, *block), F32) for _ in range(nz)] + [
+        pltpu.VMEM((nz, 12, *block), F32),
+        pltpu.VMEM((nz, 2, 2, *block), F32),
+        pltpu.VMEM(values, F32),
+        dma((nz,)),
+        dma((nz,)),
+        dma((nz, 4)),
+        dma((nz, 4)),
+        dma((nz, 4)),
+        dma((nz, 4)),
+        dma((nz, 6)),
+        dma((nz, 6)),
+        dma((4 + nz,)),
+    ]
+    operands = [asks, value, near, moved]
+    if first or FUSE:
+        scratch += [pltpu.VMEM(tiles, F32)]
+    if FUSE:
+        scratch += [pltpu.VMEM(tiles, F32)]
+    if first:
+        in_specs = [vmem, vmem, anywhere]
+        operands = operands[:3]
+        told = (nx, nz, *asks.shape)
+        out_shape += [jax.ShapeDtypeStruct(tiles, F32), jax.ShapeDtypeStruct(told, jnp.int32)]
+        out_specs += [anywhere, vmem]
+        scratch += [
+            pltpu.VMEM((nz, nx, CAP, rows, rows), F32),
+            pltpu.VMEM((nz, 2, rows, rows), F32),
+            pltpu.VMEM(told, jnp.int32),
+            pltpu.SMEM(told, jnp.int32),
             dma((nz,)),
             dma((nz,)),
-            dma((nz, 4)),
-            dma((nz, 4)),
-            dma((nz, 4)),
-            dma((nz, 4)),
             dma((nz, 6)),
             dma((nz, 6)),
+            dma((nz + nx,)),
+            dma((nz + nx,)),
             dma((nz,)),
-        ],
+        ]
+    elif not FUSE:
+        in_specs, operands = in_specs[:3] + in_specs[3:], operands
+    return pl.pallas_call(
+        functools.partial(pull_kernel, sizes, first, FUSE),
+        out_shape=out_shape,
+        in_specs=in_specs,
+        out_specs=out_specs,
+        scratch_shapes=scratch,
         compiler_params=pltpu.CompilerParams(
-            collective_id=0, has_side_effects=True, vmem_limit_bytes=48 * 2**20
+            collective_id=0 if first else 2,
+            has_side_effects=True,
+            vmem_limit_bytes=58 * 2**20,
         ),
         cost_estimate=pl.CostEstimate(
             flops=20_000_000_000, bytes_accessed=17_000_000, transcendentals=0
         ),
-        name="pull",
-    )(wanted, value)
+        name="pull_first" if first else "pull_again",
+    )(*operands)
 
 
 def scatter_kernel(ny, sums, out_ref, mated, total, early, late, cs, cr, ys, yr):
@@ -339,8 +542,10 @@
     return dot(tile_high, high) + (dot(tile_high, low) + dot(tile_low, high))
 
 
-def apply_kernel(step, target, alive, near, moved, values, sums):
+def apply_kernel(step, group, told, near, moved, values, sums):
     first = pl.program_id(0) * step
+    count = pl.num_programs(0) * step * CAP
+    me = group[0]
 
     @pl.when(first == 0)
     def _():
@@ -348,15 +553,20 @@
 
     for g in range(step):
         for slot in range(4):
-            place = (first + g) * 4 + slot
-            block = (near if slot < 2 else moved)[g, slot % 2]
-
-            @pl.when(alive[place] > 0)
-            def _(block=block, place=place, g=g, slot=slot):
-                sums[target[place]] += product(block, values[g, slot], slot >= 2)
-
-
-def apply(group_size, target, alive, near, moved, values):
+            block = (near if slot < CAP else moved)[g, slot % CAP]
+            if slot < CAP:
+                at = me * (4 * count) + (first + g) * CAP + slot
+                alive, target = told[at + 2 * count], told[at]
+            else:
+                at = (first + g) * (4 * count) + me * CAP + slot - CAP
+                alive, target = told[at + 2 * count], told[at + count]
+
+            @pl.when(alive > 0)
+            def _(block=block, target=target, g=g, slot=slot):
+                sums[target] += product(block, values[g, slot], slot >= CAP)
+
+
+def apply(group_size, group, told, near, moved, values):
     count, _, rows, width = values.shape
     step = 2
     tiles = pl.BlockSpec((step, 2, rows, rows), lambda n, *_: (n, 0, 0, 0))
@@ -380,7 +590,7 @@
             transcendentals=0,
         ),
         name="apply",
-    )(target, alive, near, moved, values)
+    )(group, told, near, moved, values)
 
 
 def exchanged(value, axis):
@@ -420,26 +630,25 @@
     alive = (slots % CAP < tile_counts[slots // CAP]).astype(jnp.int32)
     row_local = tile_rows - group * group_size
     col_local = tile_cols - slots // CAP * group_size
-    near = adj_tiles.reshape(blocks, CAP, rows, rows)
-    moved = exchanged(near, BLK)
-
-    by_group = (blocks, CAP)
-    told = exchanged(
-        jnp.concatenate([col_local.reshape(by_group), alive.reshape(by_group)], axis=1), BLK
-    )
-    direct = exchanged(col_local.reshape(nx, nz, CAP), AX)
-    turned = exchanged(row_local.reshape(nx, nz, CAP).swapaxes(0, 1), AZ).swapaxes(0, 1)
-    wanted = jnp.concatenate([direct, turned], axis=2).reshape(-1)
-    target = jnp.concatenate([row_local.reshape(by_group), told[:, :CAP]], axis=1).reshape(-1)
-    live = jnp.concatenate([alive.reshape(by_group), told[:, CAP:]], axis=1).reshape(-1)
-
-    def aggregate(value):
-        fetched = pull(sizes, wanted, value.reshape(own, rows, width))
-        sums = apply(group_size, target, live, near, moved, fetched)
-        return scatter(ny, sums).reshape(value.shape)
+    ids = jnp.concatenate([row_local, col_local, alive, alive]).reshape(2, -1)
+    near = adj_tiles.reshape(nx, nz, CAP, rows, rows)
+
+    def paired(tiles):
+        return tiles.reshape(blocks, CAP, rows, rows)
+
+    def aggregate(value, asks, moved=None):
+        pulled = pull(sizes, asks, value.reshape(own, rows, width), near, moved)
+        if moved is None:
+            fetched, moved, asks = pulled
+        else:
+            (fetched,) = pulled
+        fetched = fetched.reshape(blocks, 2 * CAP, rows, width)
+        me = group.astype(jnp.int32).reshape(1)
+        sums = apply(group_size, me, asks.reshape(-1), paired(near), paired(moved), fetched)
+        return scatter(ny, sums).reshape(value.shape), asks, moved
 
     dot = functools.partial(jnp.dot, precision=lax.Precision.HIGHEST)
-    spread = aggregate(features)
+    spread, asks, moved = aggregate(features, ids)
     pre = dot(spread, weight) + bias
     sigma = jax.nn.sigmoid(pre)
     activation = pre * sigma
@@ -448,7 +657,7 @@
         [(dot(spread.T, grad_pre) * scale).reshape(-1), jnp.sum(grad_pre, axis=0) * scale]
     )
     params = param_sum(vector)
-    grad_mixed = aggregate(grad_pre)
+    grad_mixed = aggregate(grad_pre, asks, moved)[0]
     grad_features = dot(grad_mixed, weight.T)
     grad_weight = params[: weight.size].reshape(weight.shape)
     return (activation, grad_features, grad_weight, params[weight.size :])

time: 508 us -> 440 us (0.87)
  Pallas kernels: 414 us -> 369 us
  blocking collectives: 12.6 us -> 0 us
  waiting for transfers between devices: 11.5 us -> 4.19 us
    pallas_call x2, Pallas kernels: 340 us -> 299 us  [pull(): pl.pallas_call(functools.partial(pull_kernel, sizes, first, FUSE), out_sh...]
    all_to_all x1 -> x0, blocking collectives: 12.6 us -> none  [exchanged(): return lax.all_to_all(value, axis, 0, 0, tiled=True)]
    pallas_call x2, Pallas kernels: 38.4 us -> 29.2 us  [apply(): pl.pallas_call(functools.partial(apply_kernel, step), out_shape=jax.Shape...]
    all_to_all x7 -> x4, waiting for transfers between devices: 11.5 us -> 4.19 us  [exchanged(): return lax.all_to_all(value, axis, 0, 0, tiled=True)]
    pallas_call x2, Pallas kernels: 35.4 us -> 40.6 us  [scatter(): pl.pallas_call(functools.partial(scatter_kernel, ny), out_shape=jax.Shape...]
    unnamed x18 -> x24, local copies, waits for them, and re-layouts: 11.3 us -> 16.3 us
    all_to_all x7 -> x4, starting transfers between devices: 42.1 us -> 38.9 us  [exchanged(): return lax.all_to_all(value, axis, 0, 0, tiled=True)]
  transfers between devices with their start and end apart: 7 -> 4, of which waited for: 3 -> 1; matrix products, arithmetic and copies ran while one was open for 1% -> 0% of each run, Pallas kernels for 75% -> 36%
where the time goes in v2:
time: 440 us; the launch traced here: 439 us
  Pallas kernels  369 us (84%)
  starting transfers between devices  38.9 us (9%)
  local copies, waits for them, and re-layouts  21.5 us (5%)
    pallas_call x2, Pallas kernels, pull(): pl.pallas_call(functools.partial(pull_kernel, sizes, first, FUSE), out_sh...  299 us
    pallas_call x2, Pallas kernels, scatter(): pl.pallas_call(functools.partial(scatter_kernel, ny), out_shape=jax.Shape...  40.6 us
    all_to_all x4, starting transfers between devices, exchanged(): return lax.all_to_all(value, axis, 0, 0, tiled=True)  38.9 us
    pallas_call x2, Pallas kernels, apply(): pl.pallas_call(functools.partial(apply_kernel, step), out_shape=jax.Shape...  29.2 us
    unnamed x24, local copies, waits for them, and re-layouts  16.3 us
  transfers between devices with their start and end apart: 4, of which 1 were waited for; matrix products, arithmetic and copies ran while one was open for 0% of the time, Pallas kernels for 36%

profile of v2, /device:TPU:1, one launch (start us, length us, event | category | flops | bytes accessed | tf_op | source)
XLA Modules:
  0.0 439.2 jit_solution(4520302556416579659)
XLA Ops:
  0.6 0.0 copy-start
  0.7 1.4 gather_fusion
  2.1 0.7 fusion.3
  2.8 0.6 add_bitcast_fusion.refs_0_
  3.4 172.6 %pull_first.1 = (f32[4,8,4,128,128]{4,3,2,1,0:T(8,128)}, f32[4,8,2,128,128]{4,3,2,1,0:T(8,128)}, s32[4,8,2,128]{3,2,1,0:T(2,128)}) custom-call(s32[2,128]{1,0:T(2,128)} %add_bitcast_fusion.refs_0_, f32[4,128,128]{2,1,0:T(8,128)} %bitcast.44, f32[4,8,2,128,128]{4,3,2,1,0:T(8,128)} %bitcast.27), custom_call_target="tpu_custom_call" | custom-call | flops 20000000000 | bytes 17000000 | tf_op jit(solution)/shard_map/pull_first/pallas_call | solution.py:441
  176.0 0.0 copy-start.1
  176.0 2.2 copy-done.1
  178.2 0.0 copy-start.3
  178.2 2.2 copy-done.3
  180.4 0.0 copy-start.6
  180.4 3.4 copy-done.6
  183.8 0.0 copy-start.7
  183.8 0.8 copy-done.7
  184.5 14.6 %apply.2.sums = f32[32,128,128]{2,1,0:T(8,128)S(1)} custom-call(s32[1]{0:T(128)} %bitcast.group, s32[8192]{0:T(1024)S(1)} %bitcast.38, f32[32,2,128,128]{3,2,1,0:T(8,128)S(1)} %bitcast.29, f32[32,2,128,128]{3,2,1,0:T(8,128)S(1)} %bitcast.31, f32[32,4,128,128]{3,2,1,0:T(8,128)S(1)} %bitcast.34), custom_call_target="tpu_custom_call" | custom-call | flops 1610612736 | bytes 19000000 | tf_op jit(solution)/shard_map/apply/pallas_call | solution.py:573
  199.2 0.0 copy-start.10
  199.2 0.0 copy-start.11
  199.2 21.8 %scatter.2 = f32[4,128,128]{2,1,0:T(8,128)S(1)} custom-call(f32[32,128,128]{2,1,0:T(8,128)S(1)} %apply.2.sums), custom_call_target="tpu_custom_call" | custom-call | flops 2000000000 | bytes 2000000 | tf_op jit(solution)/shard_map/scatter/pallas_call | solution.py:504
  221.0 0.0 copy-done
  221.0 0.0 copy-done.10
  221.0 0.0 copy-done.11
  221.0 1.1 fusion.5
  222.2 0.0 copy-start.9
  222.2 0.6 fusion
  222.8 0.2 reshape.122
  223.0 0.7 copy.12
  223.7 5.1 %all-to-all-start = ((f32[8,32,65]{2,1,0:T(8,128)}), f32[8,32,65]{2,1,0:T(8,128)S(1)}, u32[]{:S(2)}, u32[]{:S(2)}) async-start(f32[8,32,65]{2,1,0:T(8,128)} %copy.12), calls=%async_computation | async-start | bytes 262144 | tf_op jit(solution)/shard_map/all_to_all | solution.py:597
  228.8 0.0 copy-done.9
  228.8 0.0 copy-start.8
  228.8 126.5 %pull_again.1 = f32[4,8,4,128,128]{4,3,2,1,0:T(8,128)} custom-call(s32[4,8,2,128]{3,2,1,0:T(2,128)} %get-tuple-element.7.refs_0_, f32[4,128,128]{2,1,0:T(8,128)} %bitcast.42, f32[4,8,2,128,128]{4,3,2,1,0:T(8,128)} %bitcast.28, f32[4,8,2,128,128]{4,3,2,1,0:T(8,128)} %get-tuple-element.8.refs_3_), custom_call_target="tpu_custom_call" | custom-call | flops 20000000000 | bytes 17000000 | tf_op jit(solution)/shard_map/pull_again/pallas_call | solution.py:441
  355.3 0.0 all-to-all-done
  355.3 0.6 reduce_sum.28
  355.9 16.8 %all-to-all-start.1 = ((f32[32,1,65]{2,1,0:T(1,128)}), f32[32,1,65]{2,1,0:T(1,128)S(1)}, u32[]{:S(2)}, u32[]{:S(2)}) async-start(f32[32,1,65]{2,1,0:T(1,128)} %bitcast.15), calls=%async_computation.1 | async-start | bytes 32768 | tf_op jit(solution)/shard_map/all_to_all | solution.py:597
  372.8 0.0 copy-done.8
  372.8 0.0 copy-start.2
  372.8 2.2 copy-done.2
  375.0 0.0 copy-start.4
  375.0 2.2 copy-done.4
  377.2 0.0 copy-start.5
  377.2 3.4 copy-done.5
  380.5 14.6 %apply.3.sums = f32[32,128,128]{2,1,0:T(8,128)S(1)} custom-call(s32[1]{0:T(128)} %bitcast.group, s32[8192]{0:T(1024)S(1)} %bitcast.39, f32[32,2,128,128]{3,2,1,0:T(8,128)S(1)} %bitcast.30, f32[32,2,128,128]{3,2,1,0:T(8,128)S(1)} %bitcast.32, f32[32,4,128,128]{3,2,1,0:T(8,128)S(1)} %bitcast.33), custom_call_target="tpu_custom_call" | custom-call | flops 1610612736 | bytes 19000000 | tf_op jit(solution)/shard_map/apply/pallas_call | solution.py:573
  395.2 0.0 all-to-all-done.1
  395.2 0.1 reduce_sum.29
  395.2 0.6 broadcast_in_dim.9
  395.8 12.1 %all-to-all-start.2 = ((f32[32,1,65]{2,1,0:T(1,128)}), f32[32,1,65]{2,1,0:T(1,128)S(1)}, u32[]{:S(2)}, u32[]{:S(2)}) async-start(f32[32,1,65]{2,1,0:T(1,128)} %broadcast_in_dim.9), calls=%async_computation.2 | async-start | bytes 32768 | tf_op jit(solution)/shard_map/all_to_all | solution.py:597
  407.9 18.8 %scatter.3 = f32[4,128,128]{2,1,0:T(8,128)S(1)} custom-call(f32[32,128,128]{2,1,0:T(8,128)S(1)} %apply.3.sums), custom_call_target="tpu_custom_call" | custom-call | flops 2000000000 | bytes 2000000 | tf_op jit(solution)/shard_map/scatter/pallas_call | solution.py:504
  426.7 0.0 all-to-all-done.2
  426.7 0.7 broadcast_in_dim.22
  427.4 4.9 %all-to-all-start.3 = ((f32[8,32,65]{2,1,0:T(8,128)}), f32[8,32,65]{2,1,0:T(8,128)S(1)}, u32[]{:S(2)}, u32[]{:S(2)}) async-start(f32[8,32,65]{2,1,0:T(8,128)} %broadcast_in_dim.22), calls=%async_computation.3 | async-start | bytes 262144 | tf_op jit(solution)/shard_map/all_to_all | solution.py:597
  432.3 1.1 fusion.6
  433.4 4.2 all-to-all-done.3
  437.6 0.1 copy.13
  437.7 0.2 reshape.123
  437.9 0.2 slice.12
  438.1 0.5 slice.18
  438.6 0.6 slice.17
  (6 shorter events, 0.0 us)
Async XLA Ops:
  0.6 220.4 %copy-start = (f32[128,128]{1,0:T(8,128)S(1)}, f32[128,128]{1,0:T(8,128)}, u32[]{:S(2)}) copy-start(f32[128,128]{1,0:T(8,128)} %param.9) | copy-start | bytes 196612
  176.0 2.2 copy-start.1
  178.2 2.2 copy-start.3
  180.4 3.4 copy-start.6
  183.8 0.8 copy-start.7
  199.2 21.9 %copy-start.10 = (f32[512,128]{1,0:T(8,128)S(1)}, f32[512,128]{1,0:T(8,128)}, u32[]{:S(2)}) copy-start(f32[512,128]{1,0:T(8,128)} %param.15) | copy-start | bytes 786436
  199.2 21.9 %copy-start.11 = (f32[128]{0:T(128)S(1)}, f32[128]{0:T(128)}, u32[]{:S(2)}) copy-start(f32[128]{0:T(128)} %param.10) | copy-start | bytes 1540
  222.2 6.6 %copy-start.9 = (f32[512,128]{1,0:T(8,128)}, f32[512,128]{1,0:T(8,128)S(1)}, u32[]{:S(2)}) copy-start(f32[512,128]{1,0:T(8,128)S(1)} %get-tuple-element.11) | copy-start | bytes 786436
  223.7 131.6 %all-to-all-start = ((f32[8,32,65]{2,1,0:T(8,128)}), f32[8,32,65]{2,1,0:T(8,128)S(1)}, u32[]{:S(2)}, u32[]{:S(2)}) async-start(f32[8,32,65]{2,1,0:T(8,128)} %copy.12), calls=%async_computation | async-start | bytes 262144 | tf_op jit(solution)/shard_map/all_to_all | solution.py:597
  228.8 144.0 %copy-start.8 = (s32[4,8,2,128]{3,2,1,0:T(2,128)S(1)}, s32[4,8,2,128]{3,2,1,0:T(2,128)}, u32[]{:S(2)}) copy-start(s32[4,8,2,128]{3,2,1,0:T(2,128)} %get-tuple-element.7.refs_0_) | copy-start | bytes 98308
  355.9 39.2 %all-to-all-start.1 = ((f32[32,1,65]{2,1,0:T(1,128)}), f32[32,1,65]{2,1,0:T(1,128)S(1)}, u32[]{:S(2)}, u32[]{:S(2)}) async-start(f32[32,1,65]{2,1,0:T(1,128)} %bitcast.15), calls=%async_computation.1 | async-start | bytes 32768 | tf_op jit(solution)/shard_map/all_to_all | solution.py:597
  372.8 2.2 copy-start.2
  375.0 2.2 copy-start.4
  377.2 3.4 copy-start.5
  395.8 30.9 %all-to-all-start.2 = ((f32[32,1,65]{2,1,0:T(1,128)}), f32[32,1,65]{2,1,0:T(1,128)S(1)}, u32[]{:S(2)}, u32[]{:S(2)}) async-start(f32[32,1,65]{2,1,0:T(1,128)} %broadcast_in_dim.9), calls=%async_computation.2 | async-start | bytes 32768 | tf_op jit(solution)/shard_map/all_to_all | solution.py:597
  427.4 10.2 %all-to-all-start.3 = ((f32[8,32,65]{2,1,0:T(8,128)}), f32[8,32,65]{2,1,0:T(8,128)S(1)}, u32[]{:S(2)}, u32[]{:S(2)}) async-start(f32[8,32,65]{2,1,0:T(8,128)} %broadcast_in_dim.22), calls=%async_computation.3 | async-start | bytes 262144 | tf_op jit(solution)/shard_map/all_to_all | solution.py:597

commit v3 on v2

--- a/solution.py
+++ b/solution.py
@@ -382,7 +382,7 @@
             ids_x(d).wait_send()
 
 
-FUSE = False
+FUSE = True
 
 
 def pull(sizes, asks, value, near, moved=None):
@@ -436,8 +436,6 @@
             dma((nz + nx,)),
             dma((nz,)),
         ]
-    elif not FUSE:
-        in_specs, operands = in_specs[:3] + in_specs[3:], operands
     return pl.pallas_call(
         functools.partial(pull_kernel, sizes, first, FUSE),
         out_shape=out_shape,
@@ -542,7 +540,7 @@
     return dot(tile_high, high) + (dot(tile_high, low) + dot(tile_low, high))
 
 
-def apply_kernel(step, group, told, near, moved, values, sums):
+def add_kernel(step, group, told, products, sums):
     first = pl.program_id(0) * step
     count = pl.num_programs(0) * step * CAP
     me = group[0]
@@ -552,8 +550,7 @@
         sums[...] = jnp.zeros_like(sums)
 
     for g in range(step):
-        for slot in range(4):
-            block = (near if slot < CAP else moved)[g, slot % CAP]
+        for slot in range(2 * CAP):
             if slot < CAP:
                 at = me * (4 * count) + (first + g) * CAP + slot
                 alive, target = told[at + 2 * count], told[at]
@@ -562,35 +559,28 @@
                 alive, target = told[at + 2 * count], told[at + count]
 
             @pl.when(alive > 0)
-            def _(block=block, target=target, g=g, slot=slot):
-                sums[target] += product(block, values[g, slot], slot >= CAP)
-
-
-def apply(group_size, group, told, near, moved, values):
-    count, _, rows, width = values.shape
-    step = 2
-    tiles = pl.BlockSpec((step, 2, rows, rows), lambda n, *_: (n, 0, 0, 0))
+            def _(target=target, g=g, slot=slot):
+                sums[target] += products[g, slot]
+
+
+def add(group_size, group, told, products):
+    count, slots, rows, width = products.shape
+    step = 4
     return pl.pallas_call(
-        functools.partial(apply_kernel, step),
+        functools.partial(add_kernel, step),
         out_shape=jax.ShapeDtypeStruct((group_size, rows, width), F32),
         grid_spec=pltpu.PrefetchScalarGridSpec(
             num_scalar_prefetch=2,
             grid=(count // step,),
-            in_specs=[
-                tiles,
-                tiles,
-                pl.BlockSpec((step, 4, rows, width), lambda n, *_: (n, 0, 0, 0)),
-            ],
+            in_specs=[pl.BlockSpec((step, slots, rows, width), lambda n, *_: (n, 0, 0, 0))],
             out_specs=pl.BlockSpec((group_size, rows, width), lambda n, *_: (0, 0, 0)),
         ),
-        compiler_params=pltpu.CompilerParams(vmem_limit_bytes=24 * 2**20),
+        compiler_params=pltpu.CompilerParams(vmem_limit_bytes=58 * 2**20),
         cost_estimate=pl.CostEstimate(
-            flops=count * 4 * 6 * rows * rows * width,
-            bytes_accessed=19_000_000,
-            transcendentals=0,
+            flops=count * slots * rows * width, bytes_accessed=11_000_000, transcendentals=0
         ),
-        name="apply",
-    )(group, told, near, moved, values)
+        name="add",
+    )(group, told, products)
 
 
 def exchanged(value, axis):
@@ -633,18 +623,15 @@
     ids = jnp.concatenate([row_local, col_local, alive, alive]).reshape(2, -1)
     near = adj_tiles.reshape(nx, nz, CAP, rows, rows)
 
-    def paired(tiles):
-        return tiles.reshape(blocks, CAP, rows, rows)
-
     def aggregate(value, asks, moved=None):
         pulled = pull(sizes, asks, value.reshape(own, rows, width), near, moved)
         if moved is None:
-            fetched, moved, asks = pulled
+            products, moved, asks = pulled
         else:
-            (fetched,) = pulled
-        fetched = fetched.reshape(blocks, 2 * CAP, rows, width)
+            (products,) = pulled
+        products = products.reshape(blocks, 2 * CAP, rows, width)
         me = group.astype(jnp.int32).reshape(1)
-        sums = apply(group_size, me, asks.reshape(-1), paired(near), paired(moved), fetched)
+        sums = add(group_size, me, asks.reshape(-1), products)
         return scatter(ny, sums).reshape(value.shape), asks, moved
 
     dot = functools.partial(jnp.dot, precision=lax.Precision.HIGHEST)

time: 440 us -> 407 us (0.925)
  Pallas kernels: 369 us -> 352 us
  local copies, waits for them, and re-layouts: 21.5 us -> 7.76 us
  starting transfers between devices: 38.9 us -> 28.1 us
  blocking collectives: 0 us -> 8.74 us
    unnamed x24 -> x12, local copies, waits for them, and re-layouts: 16.3 us -> 3.2 us
    pallas_call x2, Pallas kernels: 29.2 us -> 17.7 us  [add(): pl.pallas_call(functools.partial(add_kernel, step), out_shape=jax.ShapeDt...]
    all_to_all x4 -> x3, starting transfers between devices: 38.9 us -> 28.1 us  [exchanged(): return lax.all_to_all(value, axis, 0, 0, tiled=True)]
    all_to_all x0 -> x1, blocking collectives: none -> 8.74 us  [exchanged(): return lax.all_to_all(value, axis, 0, 0, tiled=True)]
    pallas_call x2, Pallas kernels: 40.6 us -> 34 us  [scatter(): pl.pallas_call(functools.partial(scatter_kernel, ny), out_shape=jax.Shape...]
  transfers between devices with their start and end apart: 4 -> 3, of which waited for: 1 -> 1; matrix products, arithmetic and copies ran while one was open for 0% -> 0% of each run, Pallas kernels for 36% -> 38%
where the time goes in v3:
time: 407 us; the launch traced here: 406 us
  Pallas kernels  352 us (86%)
  starting transfers between devices  28.1 us (7%)
  blocking collectives  8.74 us (2%)
  local copies, waits for them, and re-layouts  7.76 us (2%)
  waiting for transfers between devices  4.19 us (1%)
    pallas_call x2, Pallas kernels, pull(): pl.pallas_call(functools.partial(pull_kernel, sizes, first, FUSE), out_sh...  300 us
    pallas_call x2, Pallas kernels, scatter(): pl.pallas_call(functools.partial(scatter_kernel, ny), out_shape=jax.Shape...  34 us
    all_to_all x3, starting transfers between devices, exchanged(): return lax.all_to_all(value, axis, 0, 0, tiled=True)  28.1 us
    pallas_call x2, Pallas kernels, add(): pl.pallas_call(functools.partial(add_kernel, step), out_shape=jax.ShapeDt...  17.7 us
    all_to_all x1, blocking collectives, exchanged(): return lax.all_to_all(value, axis, 0, 0, tiled=True)  8.74 us
  transfers between devices with their start and end apart: 3, of which 1 were waited for; matrix products, arithmetic and copies ran while one was open for 0% of the time, Pallas kernels for 38%

profile of v3, /device:TPU:1, one launch (start us, length us, event | category | flops | bytes accessed | tf_op | source)
XLA Modules:
  0.0 406.2 jit_solution(9763118451503300460)
XLA Ops:
  0.6 0.0 copy-start
  0.7 1.4 gather_fusion
  2.1 0.7 fusion.3
  2.8 0.6 add_bitcast_fusion.refs_0_
  3.4 173.5 %pull_first.1 = (f32[4,8,4,128,128]{4,3,2,1,0:T(8,128)}, f32[4,8,2,128,128]{4,3,2,1,0:T(8,128)}, s32[4,8,2,128]{3,2,1,0:T(2,128)}) custom-call(s32[2,128]{1,0:T(2,128)} %add_bitcast_fusion.refs_0_, f32[4,128,128]{2,1,0:T(8,128)} %bitcast.38, f32[4,8,2,128,128]{4,3,2,1,0:T(8,128)} %bitcast.36), custom_call_target="tpu_custom_call" | custom-call | flops 20000000000 | bytes 17000000 | tf_op jit(solution)/shard_map/pull_first/pallas_call | solution.py:439
  176.9 8.8 %add.72.sums = f32[32,128,128]{2,1,0:T(8,128)} custom-call(s32[1]{0:T(128)} %bitcast.group, s32[8192]{0:T(1024)} %bitcast.33, f32[32,4,128,128]{3,2,1,0:T(8,128)} %bitcast.28), custom_call_target="tpu_custom_call" | custom-call | flops 2097152 | bytes 11000000 | tf_op jit(solution)/shard_map/add/pallas_call | solution.py:569
  185.7 0.0 copy-start.2
  185.7 1.6 copy-done.2
  187.3 0.0 copy-start.4
  187.3 0.0 copy-start.5
  187.3 16.9 %scatter.2 = f32[4,128,128]{2,1,0:T(8,128)S(1)} custom-call(f32[32,128,128]{2,1,0:T(8,128)S(1)} %copy-done.2), custom_call_target="tpu_custom_call" | custom-call | flops 2000000000 | bytes 2000000 | tf_op jit(solution)/shard_map/scatter/pallas_call | solution.py:502
  204.2 0.0 copy-done
  204.2 0.0 copy-done.4
  204.2 0.0 copy-done.5
  204.2 1.1 fusion.5
  205.4 0.0 copy-start.3
  205.4 0.6 fusion
  206.0 0.2 reshape.117
  206.3 8.7 %all_to_all.25 = f32[8,32,65]{2,1,0:T(8,128)S(1)} all-to-all(f32[8,32,65]{2,1,0:T(8,128)S(1)} %copy.12), channel_id=1, replica_groups=mesh['blk_0'=4,'blk_1'=8,'sub_0'=4,'sub_1'=2] {'sub_0','sub_1'}, dimensions={0} | all-to-all | bytes 133120 | tf_op jit(solution)/shard_map/all_to_all | solution.py:587
  215.0 0.6 reduce_sum.28
  215.6 17.2 %all-to-all-start.1 = ((f32[32,1,65]{2,1,0:T(1,128)}), f32[32,1,65]{2,1,0:T(1,128)S(1)}, u32[]{:S(2)}, u32[]{:S(2)}) async-start(f32[32,1,65]{2,1,0:T(1,128)} %bitcast.13), calls=%async_computation.1 | async-start | bytes 32768 | tf_op jit(solution)/shard_map/all_to_all | solution.py:587
  232.8 0.0 copy-done.3
  232.8 126.6 %pull_again.1 = f32[4,8,4,128,128]{4,3,2,1,0:T(8,128)} custom-call(s32[4,8,2,128]{3,2,1,0:T(2,128)} %get-tuple-element.7.refs_0_, f32[4,128,128]{2,1,0:T(8,128)} %bitcast.32, f32[4,8,2,128,128]{4,3,2,1,0:T(8,128)} %bitcast.37, f32[4,8,2,128,128]{4,3,2,1,0:T(8,128)} %get-tuple-element.9.refs_3_), custom_call_target="tpu_custom_call" | custom-call | flops 20000000000 | bytes 17000000 | tf_op jit(solution)/shard_map/pull_again/pallas_call | solution.py:439
  359.5 8.8 %add.73.sums = f32[32,128,128]{2,1,0:T(8,128)} custom-call(s32[1]{0:T(128)} %bitcast.group, s32[8192]{0:T(1024)} %bitcast.34, f32[32,4,128,128]{3,2,1,0:T(8,128)} %bitcast.29), custom_call_target="tpu_custom_call" | custom-call | flops 2097152 | bytes 11000000 | tf_op jit(solution)/shard_map/add/pallas_call | solution.py:569
  368.3 0.0 all-to-all-done.1
  368.3 0.1 reduce_sum.29
  368.4 0.6 broadcast_in_dim.9
  369.0 6.7 %all-to-all-start.2 = ((f32[32,1,65]{2,1,0:T(1,128)}), f32[32,1,65]{2,1,0:T(1,128)S(1)}, u32[]{:S(2)}, u32[]{:S(2)}) async-start(f32[32,1,65]{2,1,0:T(1,128)} %broadcast_in_dim.9), calls=%async_computation.2 | async-start | bytes 32768 | tf_op jit(solution)/shard_map/all_to_all | solution.py:587
  375.6 0.0 copy-start.1
  375.7 1.6 copy-done.1
  377.2 17.1 %scatter.3 = f32[4,128,128]{2,1,0:T(8,128)S(1)} custom-call(f32[32,128,128]{2,1,0:T(8,128)S(1)} %copy-done.1), custom_call_target="tpu_custom_call" | custom-call | flops 2000000000 | bytes 2000000 | tf_op jit(solution)/shard_map/scatter/pallas_call | solution.py:502
  394.3 0.0 all-to-all-done.2
  394.4 0.7 broadcast_in_dim.22
  395.0 4.2 %all-to-all-start.3 = ((f32[8,32,65]{2,1,0:T(8,128)}), f32[8,32,65]{2,1,0:T(8,128)S(1)}, u32[]{:S(2)}, u32[]{:S(2)}) async-start(f32[8,32,65]{2,1,0:T(8,128)} %broadcast_in_dim.22), calls=%async_computation.3 | async-start | bytes 262144 | tf_op jit(solution)/shard_map/all_to_all | solution.py:587
  399.3 1.1 fusion.6
  400.3 4.2 %all-to-all-done.3 = f32[8,32,65]{2,1,0:T(8,128)S(1)} async-done(((f32[8,32,65]{2,1,0:T(8,128)}), f32[8,32,65]{2,1,0:T(8,128)S(1)}, u32[]{:S(2)}, u32[]{:S(2)}) %all-to-all-start.3) | async-done | bytes 66592 | tf_op jit(solution)/shard_map/all_to_all | solution.py:587
  404.5 0.1 copy.13
  404.6 0.2 slice.12
  404.8 0.2 reshape.118
  405.0 0.6 slice.17
  405.7 0.5 slice.18
  (7 shorter events, 0.1 us)
Async XLA Ops:
  0.6 203.6 %copy-start = (f32[128,128]{1,0:T(8,128)S(1)}, f32[128,128]{1,0:T(8,128)}, u32[]{:S(2)}) copy-start(f32[128,128]{1,0:T(8,128)} %param.9) | copy-start | bytes 196612
  185.7 1.6 copy-start.2
  187.3 16.9 %copy-start.4 = (f32[512,128]{1,0:T(8,128)S(1)}, f32[512,128]{1,0:T(8,128)}, u32[]{:S(2)}) copy-start(f32[512,128]{1,0:T(8,128)} %param.15) | copy-start | bytes 786436
  187.3 16.9 %copy-start.5 = (f32[128]{0:T(128)S(1)}, f32[128]{0:T(128)}, u32[]{:S(2)}) copy-start(f32[128]{0:T(128)} %param.10) | copy-start | bytes 1540
  205.4 27.4 %copy-start.3 = (f32[512,128]{1,0:T(8,128)}, f32[512,128]{1,0:T(8,128)S(1)}, u32[]{:S(2)}) copy-start(f32[512,128]{1,0:T(8,128)S(1)} %get-tuple-element.11) | copy-start | bytes 786436
  215.6 152.7 %all-to-all-start.1 = ((f32[32,1,65]{2,1,0:T(1,128)}), f32[32,1,65]{2,1,0:T(1,128)S(1)}, u32[]{:S(2)}, u32[]{:S(2)}) async-start(f32[32,1,65]{2,1,0:T(1,128)} %bitcast.13), calls=%async_computation.1 | async-start | bytes 32768 | tf_op jit(solution)/shard_map/all_to_all | solution.py:587
  369.0 25.4 %all-to-all-start.2 = ((f32[32,1,65]{2,1,0:T(1,128)}), f32[32,1,65]{2,1,0:T(1,128)S(1)}, u32[]{:S(2)}, u32[]{:S(2)}) async-start(f32[32,1,65]{2,1,0:T(1,128)} %broadcast_in_dim.9), calls=%async_computation.2 | async-start | bytes 32768 | tf_op jit(solution)/shard_map/all_to_all | solution.py:587
  375.6 1.6 copy-start.1
  395.0 9.5 %all-to-all-start.3 = ((f32[8,32,65]{2,1,0:T(8,128)}), f32[8,32,65]{2,1,0:T(8,128)S(1)}, u32[]{:S(2)}, u32[]{:S(2)}) async-start(f32[8,32,65]{2,1,0:T(8,128)} %broadcast_in_dim.22), calls=%async_computation.3 | async-start | bytes 262144 | tf_op jit(solution)/shard_map/all_to_all | solution.py:587

commit v4 on v3

--- a/solution.py
+++ b/solution.py
@@ -56,8 +56,8 @@
         ids_ref, own_ref, near_ref = take(3)
         out_ref, moved_ref, told_ref = take(3)
     else:
-        asks, own_ref, near_ref, moved_ref = take(4)
-        (out_ref,) = take(1)
+        asks, own_ref, near_ref, moved_ref, terms_ref = take(5)
+        out_ref, whole_ref = take(2)
     groups = take(nz)
     picks, relays, landing = take(3)
     zs, zr, ys, yr, cs, cr, xs, xr, ls = take(9)
@@ -68,6 +68,8 @@
     if first:
         passing, tossed, table, asks = take(4)
         ts, tr, us, ur, js, jr, ms = take(7)
+    else:
+        cut, stack, pile, joined, ps, pr = take(6)
     own = own_ref.shape[0]
     half = own // 2
     x, z, y, c = (lax.axis_index(a) for a in (AX, AZ, AY, AC))
@@ -89,25 +91,20 @@
         return copy_to(mine((j + 1) % nz), part(j, 0, c), zs, zr, j, down)
 
     def along_y(j, kind):
-        if kind == 0:
-            return copy_to(mine(j), part(j, 0, c), ys, yr, (j, 0), fore)
-        if kind == 1:
-            return copy_to(mine(j), part(j, 0, c), ys, yr, (j, 1), back)
         if kind == 2:
             piece = part(j, -1, c, 0, half)
             return copy_to(piece, piece, ys, yr, (j, 2), fore)
-        piece = part(j, 1, c, half, half)
-        return copy_to(piece, piece, ys, yr, (j, 3), back)
+        if kind == 3:
+            piece = part(j, 1, c, half, half)
+            return copy_to(piece, piece, ys, yr, (j, 3), back)
+        start = 0 if kind in (0, 5) else half
+        source = own_ref.at[pl.ds(start, half)] if j == 0 else part(j, 0, c, start, half)
+        where = fore if kind in (0, 4) else back
+        return copy_to(source, part(j, 0, c, start, half), ys, yr, (j, kind), where)
 
     def landed_y(j, kind):
-        if kind == 0:
-            piece = part(j, -1, c)
-        elif kind == 1:
-            piece = part(j, 1, c)
-        elif kind == 2:
-            piece = part(j, 2, c, 0, half)
-        else:
-            piece = part(j, 2, c, half, half)
+        away = (-1, 1, 2, 2, -1, 1)[kind]
+        piece = part(j, away, c, 0 if kind in (0, 2, 5) else half, half)
         copy_to(piece, piece, ys, yr, (j, kind), fore).wait_recv()
 
     def to_mate(j, kind):
@@ -203,6 +200,57 @@
     def moved_out(j):
         return pltpu.make_async_copy(moved.at[:, far(j)], moved_ref.at[:, far(j)], ms.at[j])
 
+    nsub = 2 * ny
+    sub = y * 2 + c
+
+    def sub_place(d):
+        there = (sub + d) % nsub
+        return {AY: there // 2, AC: there % 2}
+
+    def term(stage, d):
+        if stage == 0:
+            source = terms_ref.at[(sub + d) % nsub]
+            return copy_to(source, cut.at[sub], ps, pr, d, sub_place(d))
+        if stage == 1:
+            return copy_to(stack.at[z], stack.at[z], ps, pr, nsub + d, {AZ: (z + d) % nz})
+        at = nsub + nz + d
+        if stage == 2:
+            return copy_to(pile.at[x], pile.at[x], ps, pr, at, {AX: (x + d) % nx})
+        return copy_to(joined.at[sub], joined.at[sub], ps, pr, at + nx, sub_place(d))
+
+    def term_landed(stage, d):
+        back_by = lambda me, count: (me + count - d) % count
+        if stage == 0:
+            piece, at = cut.at[back_by(sub, nsub)], d
+        elif stage == 1:
+            piece, at = stack.at[back_by(z, nz)], nsub + d
+        elif stage == 2:
+            piece, at = pile.at[back_by(x, nx)], nsub + nz + d
+        else:
+            piece, at = joined.at[back_by(sub, nsub)], nsub + nz + nx + d
+        copy_to(piece, piece, ps, pr, at, mate).wait_recv()
+
+    def terms_in(stage):
+        return range(1, (nsub, nz, nx, nsub)[stage])
+
+    def send_terms(stage):
+        for d in terms_in(stage):
+            term(stage, d).start()
+
+    def sum_terms(stage):
+        for d in terms_in(stage):
+            term_landed(stage, d)
+        source, count = ((cut, nsub), (stack, nz), (pile, nx))[stage]
+        total = source[0]
+        for k in range(1, count):
+            total = total + source[k]
+        if stage == 0:
+            stack[z] = total
+        elif stage == 1:
+            pile[x] = total
+        else:
+            joined[sub] = total
+
     order = visiting_order(nz)
     here = {0}
 
@@ -228,8 +276,8 @@
 
     def spread(j):
         await_z(j)
-        along_y(j, 0).start()
-        along_y(j, 1).start()
+        for kind in (0, 1, 4, 5):
+            along_y(j, kind).start()
         to_mate(j, 0).start()
 
     def pass_on(j):
@@ -237,7 +285,9 @@
         along_y(j, 2).start()
         landed_y(j, 1)
         along_y(j, 3).start()
+        landed_y(j, 4)
         to_mate(j, 1).start()
+        landed_y(j, 5)
         to_mate(j, 2).start()
         landed_y(j, 2)
         landed_y(j, 3)
@@ -267,10 +317,9 @@
     def answer(j):
         for kind in (2, 3, 0, 1):
             along_x(j, kind).start()
-        if first:
-            if j:
-                tiles_z(j).wait_recv()
-                moved[x, far(j)] = passing[j, x]
+        if first and j:
+            tiles_z(j).wait_recv()
+            moved[x, far(j)] = passing[j, x]
             for kind in (2, 3, 0, 1):
                 tiles_x(j, kind).start()
 
@@ -307,10 +356,18 @@
     places = [east, west, up, down, fore, back, mate]
     if first:
         places += [{AX: (x + 2) % nx}] + [{AZ: (z + d) % nz} for d in range(2, nz - 1)]
+    else:
+        places = [{AX: (x + d) % nx} for d in range(1, nx)]
+        places += [{AZ: (z + d) % nz} for d in range(1, nz)]
+        places += [sub_place(d) for d in range(1, nsub)]
     greet(places)
+    if not first:
+        send_terms(0)
     if first:
         for d in range(1, nz):
             ids_z(d).start()
+        for kind in (2, 3, 0, 1):
+            tiles_x(0, kind).start()
     z_step(0)
     spread(0)
     if first:
@@ -318,6 +375,7 @@
         table[x, z] = ids_ref[...]
     elif fuse:
         all_moved().start()
+        cut[sub] = terms_ref[sub]
     if fuse:
         all_near().start()
     groups[0][pl.ds((y * 2 + c) * own, own)] = own_ref[...]
@@ -328,6 +386,7 @@
             copy_to(table.at[x, far(d)], table.at[x, far(d)], js, jr, d, up).wait_recv()
         for d in range(1, nx):
             ids_x(d).start()
+    stages = (1, 3, 5)
     for n, j in enumerate(order):
         pass_on(j)
         if n == 0:
@@ -342,6 +401,8 @@
             if fuse:
                 all_near().wait()
         pick(j)
+        if not first and n in stages:
+            sum_terms(stages.index(n))
         if n + 2 < nz:
             spread(order[n + 2])
         if n + 2 < nz // 2:
@@ -353,6 +414,8 @@
             tile_step(n + 1)
         if n:
             relay(order[n - 1])
+        if not first and n in stages:
+            send_terms(stages.index(n) + 1)
         answer(j)
         if n > 1:
             finish(order[n - 2])
@@ -361,14 +424,21 @@
     finish(order[-1])
     if first:
         told_ref[...] = table[...]
+    else:
+        for d in terms_in(3):
+            term_landed(3, d)
+        whole_ref[...] = joined[...]
+        for stage in range(4):
+            for d in terms_in(stage):
+                term(stage, d).wait_send()
     for j in order:
         results(j).wait()
         if j:
             along_z(j).wait_send()
         for kind in range(4):
-            along_y(j, kind).wait_send()
             to_mate(j, kind).wait_send()
         for kind in range(6):
+            along_y(j, kind).wait_send()
             along_x(j, kind).wait_send()
         if first:
             moved_out(j).wait()
@@ -385,7 +455,7 @@
 FUSE = True
 
 
-def pull(sizes, asks, value, near, moved=None):
+def pull(sizes, asks, value, near, moved=None, terms=None):
     nx, nz, ny = sizes
     first = moved is None
     own, rows, width = value.shape
@@ -397,22 +467,22 @@
     smem = pl.BlockSpec(memory_space=pltpu.SMEM)
     out_shape = [jax.ShapeDtypeStruct(values, F32)]
     out_specs = [anywhere]
-    in_specs = [smem, vmem, anywhere, anywhere]
+    in_specs = [smem, vmem, anywhere, anywhere, vmem]
     scratch = [pltpu.VMEM((ny * 2 * own, *block), F32) for _ in range(nz)] + [
         pltpu.VMEM((nz, 12, *block), F32),
         pltpu.VMEM((nz, 2, 2, *block), F32),
         pltpu.VMEM(values, F32),
         dma((nz,)),
         dma((nz,)),
-        dma((nz, 4)),
-        dma((nz, 4)),
+        dma((nz, 6)),
+        dma((nz, 6)),
         dma((nz, 4)),
         dma((nz, 4)),
         dma((nz, 6)),
         dma((nz, 6)),
         dma((4 + nz,)),
     ]
-    operands = [asks, value, near, moved]
+    operands = [asks, value, near, moved, terms]
     if first or FUSE:
         scratch += [pltpu.VMEM(tiles, F32)]
     if FUSE:
@@ -435,6 +505,17 @@
             dma((nz + nx,)),
             dma((nz + nx,)),
             dma((nz,)),
+        ]
+    else:
+        out_shape += [jax.ShapeDtypeStruct(terms.shape, F32)]
+        out_specs += [vmem]
+        scratch += [
+            pltpu.VMEM(terms.shape, F32),
+            pltpu.VMEM((nz, *terms.shape[1:]), F32),
+            pltpu.VMEM((nx, *terms.shape[1:]), F32),
+            pltpu.VMEM(terms.shape, F32),
+            dma((4 * ny + nz + nx,)),
+            dma((4 * ny + nz + nx,)),
         ]
     return pl.pallas_call(
         functools.partial(pull_kernel, sizes, first, FUSE),
@@ -583,30 +664,6 @@
     )(group, told, products)
 
 
-def exchanged(value, axis):
-    return lax.all_to_all(value, axis, 0, 0, tiled=True)
-
-
-def far_sum(pieces, axis):
-    return exchanged(pieces, axis).sum(axis=0)
-
-
-def for_each(value, axis):
-    peers = lax.axis_size(axis)
-    return exchanged(jnp.broadcast_to(value[None], (peers, *value.shape)), axis)
-
-
-def param_sum(vector):
-    blocks, subs = lax.axis_size(BLK), lax.axis_size((AY, AC))
-    spare = -vector.shape[0] % (blocks * subs)
-    padded = jnp.concatenate([vector, jnp.zeros((spare,), F32)]).reshape(blocks, subs, -1)
-    near = far_sum(padded.swapaxes(0, 1), (AY, AC))
-    done = far_sum(near, BLK)
-    line = for_each(done, BLK)
-    whole = for_each(line, (AY, AC))
-    return whole.swapaxes(0, 1).reshape(-1)[: vector.shape[0]]
-
-
 def body(features, weight, bias, adj_tiles, tile_rows, tile_cols, tile_counts, cotangent):
     nx, nz, ny = (lax.axis_size(a) for a in (AX, AZ, AY))
     sizes = (nx, nz, ny)
@@ -623,31 +680,33 @@
     ids = jnp.concatenate([row_local, col_local, alive, alive]).reshape(2, -1)
     near = adj_tiles.reshape(nx, nz, CAP, rows, rows)
 
-    def aggregate(value, asks, moved=None):
-        pulled = pull(sizes, asks, value.reshape(own, rows, width), near, moved)
-        if moved is None:
-            products, moved, asks = pulled
-        else:
-            (products,) = pulled
+    def collect(products, asks, shape):
+        me = group.astype(jnp.int32).reshape(1)
         products = products.reshape(blocks, 2 * CAP, rows, width)
-        me = group.astype(jnp.int32).reshape(1)
-        sums = add(group_size, me, asks.reshape(-1), products)
-        return scatter(ny, sums).reshape(value.shape), asks, moved
+        return scatter(ny, add(group_size, me, asks.reshape(-1), products)).reshape(shape)
 
     dot = functools.partial(jnp.dot, precision=lax.Precision.HIGHEST)
-    spread, asks, moved = aggregate(features, ids)
+    cut = (own, rows, width)
+    products, moved, asks = pull(sizes, ids, features.reshape(cut), near)
+    spread = collect(products, asks, features.shape)
     pre = dot(spread, weight) + bias
     sigma = jax.nn.sigmoid(pre)
     activation = pre * sigma
     grad_pre = cotangent * sigma * (1.0 + pre * (1.0 - sigma))
-    vector = jnp.concatenate(
-        [(dot(spread.T, grad_pre) * scale).reshape(-1), jnp.sum(grad_pre, axis=0) * scale]
-    )
-    params = param_sum(vector)
-    grad_mixed = aggregate(grad_pre, asks, moved)[0]
+    pieces = 2 * ny
+    spare = -(weight.shape[0] + 1) % (8 * pieces)
+    terms = jnp.concatenate(
+        [
+            dot(spread.T, grad_pre) * scale,
+            jnp.sum(grad_pre, axis=0)[None] * scale,
+            jnp.zeros((spare, width), F32),
+        ]
+    ).reshape(pieces, -1, width)
+    products, params = pull(sizes, asks, grad_pre.reshape(cut), near, moved, terms)
+    grad_mixed = collect(products, asks, features.shape)
     grad_features = dot(grad_mixed, weight.T)
-    grad_weight = params[: weight.size].reshape(weight.shape)
-    return (activation, grad_features, grad_weight, params[weight.size :])
+    params = params.reshape(-1, width)
+    return (activation, grad_features, params[: weight.shape[0]], params[weight.shape[0]])
 
 
 def solution(mesh):

time: 407 us -> 376 us (0.924)
  starting transfers between devices: 28.1 us -> 0 us
  Pallas kernels: 352 us -> 364 us
  blocking collectives: 8.74 us -> 0 us
  waiting for transfers between devices: 4.19 us -> 0 us
    all_to_all x3 -> x0, starting transfers between devices: 28.1 us -> none  [exchanged(): return lax.all_to_all(value, axis, 0, 0, tiled=True)]
    pallas_call x2, Pallas kernels: 300 us -> 313 us  [pull(): pl.pallas_call(functools.partial(pull_kernel, sizes, first, FUSE), out_sh...]
    all_to_all x1 -> x0, blocking collectives: 8.74 us -> none  [exchanged(): return lax.all_to_all(value, axis, 0, 0, tiled=True)]
    all_to_all x3 -> x0, waiting for transfers between devices: 4.19 us -> none  [exchanged(): return lax.all_to_all(value, axis, 0, 0, tiled=True)]
  transfers between devices with their start and end apart: 3 -> 0, of which waited for: 1 -> 0; matrix products, arithmetic and copies ran while one was open for 0% -> 0% of each run, Pallas kernels for 38% -> 0%
where the time goes in v4:
time: 376 us
  Pallas kernels  364 us (97%)
  local copies, waits for them, and re-layouts  5.86 us (2%)
    pallas_call x2, Pallas kernels, pull(): pl.pallas_call(functools.partial(pull_kernel, sizes, first, FUSE), out_sh...  313 us
    pallas_call x2, Pallas kernels, scatter(): pl.pallas_call(functools.partial(scatter_kernel, ny), out_shape=jax.Shape...  33.5 us
    pallas_call x2, Pallas kernels, add(): pl.pallas_call(functools.partial(add_kernel, step), out_shape=jax.ShapeDt...  17.6 us

profile of v4, /device:TPU:1, one launch (start us, length us, event | category | flops | bytes accessed | tf_op | source)
XLA Modules:
  0.0 375.6 jit_solution(1541564064257268543)
XLA Ops:
  0.6 0.0 copy-start
  0.7 0.7 fusion.2
  1.4 1.4 gather_fusion
  2.8 0.6 add_bitcast_fusion.refs_0_
  3.5 173.6 %pull_first.1 = (f32[4,8,4,128,128]{4,3,2,1,0:T(8,128)}, f32[4,8,2,128,128]{4,3,2,1,0:T(8,128)}, s32[4,8,2,128]{3,2,1,0:T(2,128)}) custom-call(s32[2,128]{1,0:T(2,128)} %add_bitcast_fusion.refs_0_, f32[4,128,128]{2,1,0:T(8,128)} %bitcast.38, f32[4,8,2,128,128]{4,3,2,1,0:T(8,128)} %bitcast.36), custom_call_target="tpu_custom_call" | custom-call | flops 20000000000 | bytes 17000000 | tf_op jit(solution)/shard_map/pull_first/pallas_call | solution.py:520
  177.1 8.8 %add.72.sums = f32[32,128,128]{2,1,0:T(8,128)} custom-call(s32[1]{0:T(128)} %bitcast.group, s32[8192]{0:T(1024)} %bitcast.31, f32[32,4,128,128]{3,2,1,0:T(8,128)} %bitcast.29), custom_call_target="tpu_custom_call" | custom-call | flops 2097152 | bytes 11000000 | tf_op jit(solution)/shard_map/add/pallas_call | solution.py:650
  185.8 0.0 copy-start.2
  185.8 1.6 copy-done.2
  187.4 0.0 copy-start.5
  187.4 0.0 copy-start.6
  187.4 17.0 %scatter.2 = f32[4,128,128]{2,1,0:T(8,128)S(1)} custom-call(f32[32,128,128]{2,1,0:T(8,128)S(1)} %copy-done.2), custom_call_target="tpu_custom_call" | custom-call | flops 2000000000 | bytes 2000000 | tf_op jit(solution)/shard_map/scatter/pallas_call | solution.py:583
  204.4 0.0 copy-done
  204.5 0.0 copy-done.5
  204.5 0.0 copy-done.6
  204.5 1.1 fusion.4
  205.6 0.0 copy-start.3
  205.6 0.6 convolution_multiply_fusion
  206.2 0.1 pad.2.clone
  206.3 0.7 maximum_maximum_fusion
  207.1 0.0 copy-done.3
  207.1 139.4 %pull_again.1 = (f32[4,8,4,128,128]{4,3,2,1,0:T(8,128)}, f32[8,24,128]{2,1,0:T(8,128)}) custom-call(s32[4,8,2,128]{3,2,1,0:T(2,128)} %get-tuple-element.9.refs_0_, f32[4,128,128]{2,1,0:T(8,128)} %bitcast.30, f32[4,8,2,128,128]{4,3,2,1,0:T(8,128)} %bitcast.37, f32[4,8,2,128,128]{4,3,2,1,0:T(8,128)} %get-tuple-element.11.refs_3_, f32[8,24,128]{2,1,0:T(8,128)} %bitcast.33), custom_call_target="tpu_custom_call" | custom-call | flops 20000000000 | bytes 17000000 | tf_op jit(solution)/shard_map/pull_again/pallas_call | solution.py:520
  346.5 8.8 %add.73.sums = f32[32,128,128]{2,1,0:T(8,128)} custom-call(s32[1]{0:T(128)} %bitcast.group, s32[8192]{0:T(1024)} %bitcast.32, f32[32,4,128,128]{3,2,1,0:T(8,128)} %bitcast.28), custom_call_target="tpu_custom_call" | custom-call | flops 2097152 | bytes 11000000 | tf_op jit(solution)/shard_map/add/pallas_call | solution.py:650
  355.3 0.0 copy-start.1
  355.3 1.6 copy-done.1
  356.9 0.0 copy-start.4
  356.9 16.5 %scatter.3 = f32[4,128,128]{2,1,0:T(8,128)S(1)} custom-call(f32[32,128,128]{2,1,0:T(8,128)S(1)} %copy-done.1), custom_call_target="tpu_custom_call" | custom-call | flops 2000000000 | bytes 2000000 | tf_op jit(solution)/shard_map/scatter/pallas_call | solution.py:583
  373.4 1.1 fusion.5
  374.5 0.0 copy-done.4
  374.5 0.6 slice.10
  375.1 0.5 slice_bitcast_fusion
  (5 shorter events, 0.0 us)
Async XLA Ops:
  0.6 203.8 %copy-start = (f32[128,128]{1,0:T(8,128)S(1)}, f32[128,128]{1,0:T(8,128)}, u32[]{:S(2)}) copy-start(f32[128,128]{1,0:T(8,128)} %param.9) | copy-start | bytes 196612
  185.8 1.6 copy-start.2
  187.4 17.1 %copy-start.5 = (f32[512,128]{1,0:T(8,128)S(1)}, f32[512,128]{1,0:T(8,128)}, u32[]{:S(2)}) copy-start(f32[512,128]{1,0:T(8,128)} %param.15) | copy-start | bytes 786436
  187.4 17.1 %copy-start.6 = (f32[128]{0:T(128)S(1)}, f32[128]{0:T(128)}, u32[]{:S(2)}) copy-start(f32[128]{0:T(128)} %param.10) | copy-start | bytes 1540
  205.6 1.4 copy-start.3
  355.3 1.6 copy-start.1
  356.9 17.6 %copy-start.4 = (f32[8,24,128]{2,1,0:T(8,128)S(1)}, f32[8,24,128]{2,1,0:T(8,128)}, u32[]{:S(2)}) copy-start(f32[8,24,128]{2,1,0:T(8,128)} %get-tuple-element.13) | copy-start | bytes 294916

commit v5 on v4

--- a/solution.py
+++ b/solution.py
@@ -280,11 +280,13 @@
             along_y(j, kind).start()
         to_mate(j, 0).start()
 
-    def pass_on(j):
+    def pass_first(j):
         landed_y(j, 0)
         along_y(j, 2).start()
         landed_y(j, 1)
         along_y(j, 3).start()
+
+    def pass_on(j):
         landed_y(j, 4)
         to_mate(j, 1).start()
         landed_y(j, 5)
@@ -379,15 +381,19 @@
     if fuse:
         all_near().start()
     groups[0][pl.ds((y * 2 + c) * own, own)] = own_ref[...]
+    pass_first(0)
     spread(order[1])
     z_step(1)
+    tile_step(1)
     if first:
         for d in range(1, nz):
             copy_to(table.at[x, far(d)], table.at[x, far(d)], js, jr, d, up).wait_recv()
         for d in range(1, nx):
             ids_x(d).start()
-    stages = (1, 3, 5)
+    stages = (1, 2, 5)
     for n, j in enumerate(order):
+        if n:
+            pass_first(j)
         pass_on(j)
         if n == 0:
             if first:
@@ -407,11 +413,11 @@
             spread(order[n + 2])
         if n + 2 < nz // 2:
             z_step(n + 2)
-        if n == 2:
+        if n == 1:
             for k in range(3, nz // 2 + 1):
                 tile_step(k)
-        elif n < 2:
-            tile_step(n + 1)
+        elif n == 0:
+            tile_step(2)
         if n:
             relay(order[n - 1])
         if not first and n in stages:
@@ -549,8 +555,13 @@
 
     early_fore = copy_to(total.at[2, pl.ds(0, half)], early.at[0], ys, yr, 0, fore)
     early_back = copy_to(total.at[2, pl.ds(half, half)], early.at[1], ys, yr, 1, back)
-    late_fore = copy_to(total.at[1], late.at[0], ys, yr, 2, fore)
-    late_back = copy_to(total.at[3], late.at[1], ys, yr, 3, back)
+
+
+    def late_copy(k, which, where):
+        piece = pl.ds((0 if which == k else half), half)
+        return copy_to(total.at[2 * k + 1, piece], late.at[k, piece], ys, yr, 2 + 2 * k + which, where)
+
+    late_fore, late_back = ([late_copy(k, w, (fore, back)[k]) for w in (0, 1)] for k in (0, 1))
     greet((fore, back, mate))
     for k in (2, 1, 3, 0):
         over(k).start()
@@ -560,18 +571,22 @@
         if k == 1:
             early_fore.start()
             early_back.start()
+        if k == 3:
+            late_fore[1].start()
+        if k == 0:
+            late_back[1].start()
     early_fore.wait_recv()
     total[1, pl.ds(0, half)] = total[1, pl.ds(0, half)] + early[0]
     early_back.wait_recv()
     total[3, pl.ds(half, half)] = total[3, pl.ds(half, half)] + early[1]
-    late_fore.start()
-    late_back.start()
-    late_fore.wait_recv()
-    late_back.wait_recv()
+    late_fore[0].start()
+    late_back[0].start()
+    for copy in late_fore + late_back:
+        copy.wait_recv()
     out_ref[...] = total[0] + late[0] + late[1]
     for k in range(4):
         over(k).wait_send()
-    for copy in (early_fore, early_back, late_fore, late_back):
+    for copy in [early_fore, early_back] + late_fore + late_back:
         copy.wait_send()
 
 
@@ -592,8 +607,8 @@
             pltpu.VMEM((2, *piece), F32),
             dma((4,)),
             dma((4,)),
-            dma((4,)),
-            dma((4,)),
+            dma((6,)),
+            dma((6,)),
         ],
         compiler_params=pltpu.CompilerParams(
             collective_id=1, has_side_effects=True, vmem_limit_bytes=16 * 2**20
@@ -621,14 +636,16 @@
     return dot(tile_high, high) + (dot(tile_high, low) + dot(tile_low, high))
 
 
-def add_kernel(step, group, told, products, sums):
+def add_kernel(step, group, told, products, sums, total):
     first = pl.program_id(0) * step
     count = pl.num_programs(0) * step * CAP
     me = group[0]
 
+    spare = sums.shape[0]
+
     @pl.when(first == 0)
     def _():
-        sums[...] = jnp.zeros_like(sums)
+        total[...] = jnp.zeros_like(total)
 
     for g in range(step):
         for slot in range(2 * CAP):
@@ -639,9 +656,12 @@
                 at = (first + g) * (4 * count) + me * CAP + slot - CAP
                 alive, target = told[at + 2 * count], told[at + count]
 
-            @pl.when(alive > 0)
-            def _(target=target, g=g, slot=slot):
-                sums[target] += products[g, slot]
+            target = jnp.where(alive > 0, target, spare)
+            total[target] += products[g, slot]
+
+    @pl.when(pl.program_id(0) == pl.num_programs(0) - 1)
+    def _():
+        sums[...] = total[pl.ds(0, spare)]
 
 
 def add(group_size, group, told, products):
@@ -655,6 +675,7 @@
             grid=(count // step,),
             in_specs=[pl.BlockSpec((step, slots, rows, width), lambda n, *_: (n, 0, 0, 0))],
             out_specs=pl.BlockSpec((group_size, rows, width), lambda n, *_: (0, 0, 0)),
+            scratch_shapes=[pltpu.VMEM((group_size + 1, rows, width), F32)],
         ),
         compiler_params=pltpu.CompilerParams(vmem_limit_bytes=58 * 2**20),
         cost_estimate=pl.CostEstimate(

time: 376 us -> 359 us (0.955)
  Pallas kernels: 364 us -> 347 us
    pallas_call x2, Pallas kernels: 313 us -> 295 us  [pull(): pl.pallas_call(functools.partial(pull_kernel, sizes, first, FUSE), out_sh...]
where the time goes in v5:
time: 359 us
  Pallas kernels  347 us (97%)
  local copies, waits for them, and re-layouts  5.86 us (2%)
    pallas_call x2, Pallas kernels, pull(): pl.pallas_call(functools.partial(pull_kernel, sizes, first, FUSE), out_sh...  295 us
    pallas_call x2, Pallas kernels, scatter(): pl.pallas_call(functools.partial(scatter_kernel, ny), out_shape=jax.Shape...  34.4 us
    pallas_call x2, Pallas kernels, add(): pl.pallas_call(functools.partial(add_kernel, step), out_shape=jax.ShapeDt...  17.6 us

profile of v5, /device:TPU:1, one launch (start us, length us, event | category | flops | bytes accessed | tf_op | source)
XLA Modules:
  0.0 358.6 jit_solution(1869475852154772)
XLA Ops:
  0.6 0.0 copy-start
  0.7 0.7 fusion.2
  1.4 1.4 gather_fusion
  2.8 0.6 add_bitcast_fusion.refs_0_
  3.5 167.1 %pull_first.1 = (f32[4,8,4,128,128]{4,3,2,1,0:T(8,128)}, f32[4,8,2,128,128]{4,3,2,1,0:T(8,128)}, s32[4,8,2,128]{3,2,1,0:T(2,128)}) custom-call(s32[2,128]{1,0:T(2,128)} %add_bitcast_fusion.refs_0_, f32[4,128,128]{2,1,0:T(8,128)} %bitcast.38, f32[4,8,2,128,128]{4,3,2,1,0:T(8,128)} %bitcast.36), custom_call_target="tpu_custom_call" | custom-call | flops 20000000000 | bytes 17000000 | tf_op jit(solution)/shard_map/pull_first/pallas_call | solution.py:526
  170.6 8.8 %add.72.sums = f32[32,128,128]{2,1,0:T(8,128)} custom-call(s32[1]{0:T(128)} %bitcast.group, s32[8192]{0:T(1024)} %bitcast.31, f32[32,4,128,128]{3,2,1,0:T(8,128)} %bitcast.29), custom_call_target="tpu_custom_call" | custom-call | flops 2097152 | bytes 11000000 | tf_op jit(solution)/shard_map/add/pallas_call | solution.py:670
  179.4 0.0 copy-start.2
  179.4 1.6 copy-done.2
  180.9 0.0 copy-start.5
  180.9 0.0 copy-start.6
  181.0 17.5 %scatter.2 = f32[4,128,128]{2,1,0:T(8,128)S(1)} custom-call(f32[32,128,128]{2,1,0:T(8,128)S(1)} %copy-done.2), custom_call_target="tpu_custom_call" | custom-call | flops 2000000000 | bytes 2000000 | tf_op jit(solution)/shard_map/scatter/pallas_call | solution.py:598
  198.4 0.0 copy-done
  198.4 0.0 copy-done.5
  198.5 0.0 copy-done.6
  198.5 1.1 fusion.4
  199.6 0.0 copy-start.3
  199.6 0.6 convolution_multiply_fusion
  200.2 0.1 pad.2.clone
  200.3 0.7 maximum_maximum_fusion
  201.0 0.0 copy-done.3
  201.0 127.9 %pull_again.1 = (f32[4,8,4,128,128]{4,3,2,1,0:T(8,128)}, f32[8,24,128]{2,1,0:T(8,128)}) custom-call(s32[4,8,2,128]{3,2,1,0:T(2,128)} %get-tuple-element.9.refs_0_, f32[4,128,128]{2,1,0:T(8,128)} %bitcast.30, f32[4,8,2,128,128]{4,3,2,1,0:T(8,128)} %bitcast.37, f32[4,8,2,128,128]{4,3,2,1,0:T(8,128)} %get-tuple-element.11.refs_3_, f32[8,24,128]{2,1,0:T(8,128)} %bitcast.33), custom_call_target="tpu_custom_call" | custom-call | flops 20000000000 | bytes 17000000 | tf_op jit(solution)/shard_map/pull_again/pallas_call | solution.py:526
  329.0 8.8 %add.73.sums = f32[32,128,128]{2,1,0:T(8,128)} custom-call(s32[1]{0:T(128)} %bitcast.group, s32[8192]{0:T(1024)} %bitcast.32, f32[32,4,128,128]{3,2,1,0:T(8,128)} %bitcast.28), custom_call_target="tpu_custom_call" | custom-call | flops 2097152 | bytes 11000000 | tf_op jit(solution)/shard_map/add/pallas_call | solution.py:670
  337.8 0.0 copy-start.1
  337.8 1.6 copy-done.1
  339.4 0.0 copy-start.4
  339.4 16.9 %scatter.3 = f32[4,128,128]{2,1,0:T(8,128)S(1)} custom-call(f32[32,128,128]{2,1,0:T(8,128)S(1)} %copy-done.1), custom_call_target="tpu_custom_call" | custom-call | flops 2000000000 | bytes 2000000 | tf_op jit(solution)/shard_map/scatter/pallas_call | solution.py:598
  356.3 1.1 fusion.5
  357.4 0.0 copy-done.4
  357.4 0.6 slice.10
  358.1 0.5 slice_bitcast_fusion
  (5 shorter events, 0.0 us)
Async XLA Ops:
  0.6 197.8 %copy-start = (f32[128,128]{1,0:T(8,128)S(1)}, f32[128,128]{1,0:T(8,128)}, u32[]{:S(2)}) copy-start(f32[128,128]{1,0:T(8,128)} %param.9) | copy-start | bytes 196612
  179.4 1.6 copy-start.2
  180.9 17.5 %copy-start.5 = (f32[512,128]{1,0:T(8,128)S(1)}, f32[512,128]{1,0:T(8,128)}, u32[]{:S(2)}) copy-start(f32[512,128]{1,0:T(8,128)} %param.15) | copy-start | bytes 786436
  180.9 17.5 %copy-start.6 = (f32[128]{0:T(128)S(1)}, f32[128]{0:T(128)}, u32[]{:S(2)}) copy-start(f32[128]{0:T(128)} %param.10) | copy-start | bytes 1540
  199.6 1.4 copy-start.3
  337.8 1.6 copy-start.1
  339.4 18.0 %copy-start.4 = (f32[8,24,128]{2,1,0:T(8,128)S(1)}, f32[8,24,128]{2,1,0:T(8,128)}, u32[]{:S(2)}) copy-start(f32[8,24,128]{2,1,0:T(8,128)} %get-tuple-element.13) | copy-start | bytes 294916

commit v6 on v5

--- a/solution.py
+++ b/solution.py
@@ -636,48 +636,47 @@
     return dot(tile_high, high) + (dot(tile_high, low) + dot(tile_low, high))
 
 
-def add_kernel(step, group, told, products, sums, total):
-    first = pl.program_id(0) * step
-    count = pl.num_programs(0) * step * CAP
+def add_kernel(group, told, products, sums, total, held, sems):
+    count, spare = held.shape[0], sums.shape[0]
+    step = count // sems.shape[0]
     me = group[0]
 
-    spare = sums.shape[0]
-
-    @pl.when(first == 0)
-    def _():
-        total[...] = jnp.zeros_like(total)
-
-    for g in range(step):
-        for slot in range(2 * CAP):
-            if slot < CAP:
-                at = me * (4 * count) + (first + g) * CAP + slot
-                alive, target = told[at + 2 * count], told[at]
-            else:
-                at = (first + g) * (4 * count) + me * CAP + slot - CAP
-                alive, target = told[at + 2 * count], told[at + count]
-
-            target = jnp.where(alive > 0, target, spare)
-            total[target] += products[g, slot]
-
-    @pl.when(pl.program_id(0) == pl.num_programs(0) - 1)
-    def _():
-        sums[...] = total[pl.ds(0, spare)]
+    def piece(k):
+        rows = pl.ds(k * step, step)
+        return pltpu.make_async_copy(products.at[rows], held.at[rows], sems.at[k])
+
+    for k in range(count // step):
+        piece(k).start()
+    total[...] = jnp.zeros_like(total)
+    for k in range(count // step):
+        piece(k).wait()
+        for g in range(k * step, k * step + step):
+            for slot in range(2 * CAP):
+                if slot < CAP:
+                    at = me * (4 * CAP * count) + g * CAP + slot
+                    alive, target = told[at + 2 * CAP * count], told[at]
+                else:
+                    at = g * (4 * CAP * count) + me * CAP + slot - CAP
+                    alive, target = told[at + 2 * CAP * count], told[at + CAP * count]
+                target = jnp.where(alive > 0, target, spare)
+                total[target] += held[g, slot]
+    sums[...] = total[pl.ds(0, spare)]
 
 
 def add(group_size, group, told, products):
     count, slots, rows, width = products.shape
-    step = 4
+    smem = pl.BlockSpec(memory_space=pltpu.SMEM)
     return pl.pallas_call(
-        functools.partial(add_kernel, step),
+        add_kernel,
         out_shape=jax.ShapeDtypeStruct((group_size, rows, width), F32),
-        grid_spec=pltpu.PrefetchScalarGridSpec(
-            num_scalar_prefetch=2,
-            grid=(count // step,),
-            in_specs=[pl.BlockSpec((step, slots, rows, width), lambda n, *_: (n, 0, 0, 0))],
-            out_specs=pl.BlockSpec((group_size, rows, width), lambda n, *_: (0, 0, 0)),
-            scratch_shapes=[pltpu.VMEM((group_size + 1, rows, width), F32)],
-        ),
-        compiler_params=pltpu.CompilerParams(vmem_limit_bytes=58 * 2**20),
+        in_specs=[smem, smem, pl.BlockSpec(memory_space=pl.ANY)],
+        out_specs=pl.BlockSpec(memory_space=pltpu.VMEM),
+        scratch_shapes=[
+            pltpu.VMEM((group_size + 1, rows, width), F32),
+            pltpu.VMEM(products.shape, F32),
+            pltpu.SemaphoreType.DMA((16,)),
+        ],
+        compiler_params=pltpu.CompilerParams(vmem_limit_bytes=57 * 2**20),
         cost_estimate=pl.CostEstimate(
             flops=count * slots * rows * width, bytes_accessed=11_000_000, transcendentals=0
         ),

time: 359 us -> 354 us (0.986)
  Pallas kernels: 347 us -> 342 us
    pallas_call x2, Pallas kernels: 17.6 us -> 12.5 us  [add(): pl.pallas_call(add_kernel, out_shape=jax.ShapeDtypeStruct((group_size, ro...]
where the time goes in v6:
time: 354 us
  Pallas kernels  342 us (97%)
  local copies, waits for them, and re-layouts  5.85 us (2%)
    pallas_call x2, Pallas kernels, pull(): pl.pallas_call(functools.partial(pull_kernel, sizes, first, FUSE), out_sh...  295 us
    pallas_call x2, Pallas kernels, scatter(): pl.pallas_call(functools.partial(scatter_kernel, ny), out_shape=jax.Shape...  34.4 us
    pallas_call x2, Pallas kernels, add(): pl.pallas_call(add_kernel, out_shape=jax.ShapeDtypeStruct((group_size, ro...  12.5 us

profile of v6, /device:TPU:1, one launch (start us, length us, event | category | flops | bytes accessed | tf_op | source)
XLA Modules:
  0.0 353.6 jit_solution(2524003377980057882)
XLA Ops:
  0.6 0.0 copy-start
  0.7 0.7 fusion.2
  1.4 1.4 gather_fusion
  2.8 0.6 add_bitcast_fusion.refs_0_
  3.5 167.1 %pull_first.1 = (f32[4,8,4,128,128]{4,3,2,1,0:T(8,128)}, f32[4,8,2,128,128]{4,3,2,1,0:T(8,128)}, s32[4,8,2,128]{3,2,1,0:T(2,128)}) custom-call(s32[2,128]{1,0:T(2,128)} %add_bitcast_fusion.refs_0_, f32[4,128,128]{2,1,0:T(8,128)} %bitcast.38, f32[4,8,2,128,128]{4,3,2,1,0:T(8,128)} %bitcast.36), custom_call_target="tpu_custom_call" | custom-call | flops 20000000000 | bytes 17000000 | tf_op jit(solution)/shard_map/pull_first/pallas_call | solution.py:526
  170.6 6.2 %add.72.sums = f32[32,128,128]{2,1,0:T(8,128)} custom-call(s32[1]{0:T(128)} %bitcast.group, s32[8192]{0:T(1024)} %bitcast.31, f32[32,4,128,128]{3,2,1,0:T(8,128)} %bitcast.29), custom_call_target="tpu_custom_call" | custom-call | flops 2097152 | bytes 11000000 | tf_op jit(solution)/shard_map/add/pallas_call | solution.py:669
  176.8 0.0 copy-start.2
  176.8 1.6 copy-done.2
  178.4 0.0 copy-start.5
  178.4 0.0 copy-start.6
  178.4 17.5 %scatter.2 = f32[4,128,128]{2,1,0:T(8,128)S(1)} custom-call(f32[32,128,128]{2,1,0:T(8,128)S(1)} %copy-done.2), custom_call_target="tpu_custom_call" | custom-call | flops 2000000000 | bytes 2000000 | tf_op jit(solution)/shard_map/scatter/pallas_call | solution.py:598
  195.9 0.0 copy-done
  195.9 0.0 copy-done.5
  195.9 0.0 copy-done.6
  195.9 1.1 fusion.4
  197.0 0.0 copy-start.3
  197.1 0.6 convolution_multiply_fusion
  197.7 0.1 pad.2.clone
  197.7 0.7 maximum_maximum_fusion
  198.5 0.0 copy-done.3
  198.5 128.1 %pull_again.1 = (f32[4,8,4,128,128]{4,3,2,1,0:T(8,128)}, f32[8,24,128]{2,1,0:T(8,128)}) custom-call(s32[4,8,2,128]{3,2,1,0:T(2,128)} %get-tuple-element.9.refs_0_, f32[4,128,128]{2,1,0:T(8,128)} %bitcast.30, f32[4,8,2,128,128]{4,3,2,1,0:T(8,128)} %bitcast.37, f32[4,8,2,128,128]{4,3,2,1,0:T(8,128)} %get-tuple-element.11.refs_3_, f32[8,24,128]{2,1,0:T(8,128)} %bitcast.33), custom_call_target="tpu_custom_call" | custom-call | flops 20000000000 | bytes 17000000 | tf_op jit(solution)/shard_map/pull_again/pallas_call | solution.py:526
  326.6 6.3 %add.73.sums = f32[32,128,128]{2,1,0:T(8,128)} custom-call(s32[1]{0:T(128)} %bitcast.group, s32[8192]{0:T(1024)} %bitcast.32, f32[32,4,128,128]{3,2,1,0:T(8,128)} %bitcast.28), custom_call_target="tpu_custom_call" | custom-call | flops 2097152 | bytes 11000000 | tf_op jit(solution)/shard_map/add/pallas_call | solution.py:669
  332.9 0.0 copy-start.1
  332.9 1.6 copy-done.1
  334.5 0.0 copy-start.4
  334.5 16.9 %scatter.3 = f32[4,128,128]{2,1,0:T(8,128)S(1)} custom-call(f32[32,128,128]{2,1,0:T(8,128)S(1)} %copy-done.1), custom_call_target="tpu_custom_call" | custom-call | flops 2000000000 | bytes 2000000 | tf_op jit(solution)/shard_map/scatter/pallas_call | solution.py:598
  351.3 1.1 fusion.5
  352.4 0.0 copy-done.4
  352.4 0.6 slice.10
  353.1 0.5 slice_bitcast_fusion
  (5 shorter events, 0.0 us)
Async XLA Ops:
  0.6 195.2 %copy-start = (f32[128,128]{1,0:T(8,128)S(1)}, f32[128,128]{1,0:T(8,128)}, u32[]{:S(2)}) copy-start(f32[128,128]{1,0:T(8,128)} %param.9) | copy-start | bytes 196612
  176.8 1.6 copy-start.2
  178.4 17.5 %copy-start.5 = (f32[512,128]{1,0:T(8,128)S(1)}, f32[512,128]{1,0:T(8,128)}, u32[]{:S(2)}) copy-start(f32[512,128]{1,0:T(8,128)} %param.15) | copy-start | bytes 786436
  178.4 17.5 %copy-start.6 = (f32[128]{0:T(128)S(1)}, f32[128]{0:T(128)}, u32[]{:S(2)}) copy-start(f32[128]{0:T(128)} %param.10) | copy-start | bytes 1540
  197.0 1.4 copy-start.3
  332.9 1.6 copy-start.1
  334.5 18.0 %copy-start.4 = (f32[8,24,128]{2,1,0:T(8,128)S(1)}, f32[8,24,128]{2,1,0:T(8,128)}, u32[]{:S(2)}) copy-start(f32[8,24,128]{2,1,0:T(8,128)} %get-tuple-element.13) | copy-start | bytes 294916
